TPU v7x, 32 devices: a whole 2x2x4 slice. The times are simulated.
32 devices in a mesh: seq: 8 (over z, x), head: 4 (over y, core).
Axes of the slice: x: 2, y: 2, z: 4, core: 2. Of those that a mesh axis runs over, the one named last changes fastest.
Arguments:
- xs: bfloat16 [8192, 4096], P('seq', 'head'), may hold values from -6 to 6
- gate_branch: bfloat16 [8192, 4096], P('seq', 'head'), may hold values from -6 to 6
- bmat: bfloat16 [8192, 128], P('seq'), may hold values from -0.375 to 0.375
- cmat: bfloat16 [8192, 128], P('seq'), may hold values from -0.375 to 0.375
- dt_code: int32 [64, 8192], P('head', 'seq'), may hold values from 1 to 32768
- resets: int32 [8192], P('seq'), may hold values 0 or 1
- decay_rate: float32 [64], P('head'), may hold values from 4.8828125e-05 to 0.08, as said below
- skip: float32 [64], P('head'), may hold values from 0.5 to 1.5
- norm_gain: float32 [4096], P('head'), may hold values from 0.1 to 1.9
- out_weight: bfloat16 [4096, 4096], P('head'), may hold values from -0.09375 to 0.09375
Outputs:
- mixed: bfloat16 [8192, 4096], P(('seq', 'head'))
Inputs may be any that keep to these rules, and one draw needn't show every extreme that they name: `decay_rate`: positive rates.
All inputs are finite; a program needn't handle non-finite values. No bound on the sum of `resets` on one device may be relied on, other than what follows from the above.
Results may differ from a plain program's by a relative error of at most 0.023.
Values may be sent and summed in bfloat16 or wider, within the bound.
No kernel may reach another device: no remote copies, remote signals or barrier semaphores. Data moves between devices by JAX's collectives and lax.ppermute only.
A program may use at most 128 MiB of HBM per device.

v0:
```python
import functools

import jax
import jax.numpy as jnp
from jax import lax
from jax.experimental import pallas as pl
from jax.experimental.pallas import tpu as pltpu
from jax.sharding import PartitionSpec as P


SPAN = 256
LANES = 128
LOG2E = 1.4426950408889634
F32 = jnp.float32
BF16 = jnp.bfloat16
PARAMS = pltpu.CompilerParams(vmem_limit_bytes=24 << 20)
WHOLE = pltpu.CompilerParams(vmem_limit_bytes=60 * 1024 * 1024)
CUTS = (1, 3, 5, 3, 3, 1)
ALONE = 3
TAIL = 8
RING = 4


def block_of(place, k, teams, i):
    team = (place[0] // 2 + k) % teams
    half = place[0] % 2
    return 2 * team + (half if i == 0 else 1 - half)


def block_cumsum(v):
    pos = lax.broadcasted_iota(jnp.int32, v.shape, 1) % SPAN
    k = 1
    while k < SPAN:
        v = v + jnp.where(pos >= k, pltpu.roll(v, k, 1), 0.0)
        k *= 2
    return v


def column_of(row):
    n = row.shape[1]
    at = lax.broadcasted_iota(jnp.int32, (n, n), 0) == lax.broadcasted_iota(jnp.int32, (n, n), 1)
    return jnp.sum(jnp.where(at, jnp.broadcast_to(row, (n, n)), 0.0), axis=1, keepdims=True)


def where_am_i():
    shard = lax.axis_index("seq")
    return lax.axis_index("head"), shard & (RING - 1), shard >> (RING.bit_length() - 1)


def prep(dt, rate, resets):
    step = dt.astype(F32) / 16.0
    scale = jnp.minimum(step, 1.0)
    cum = block_cumsum((-LOG2E * column_of(rate)) * step)
    count = block_cumsum(jnp.broadcast_to(resets.astype(F32), (8, resets.shape[1])))
    return scale, cum, count


def halves(first, second, shape, width):
    lane = lax.broadcasted_iota(jnp.int32, shape, 1) % LANES
    return jnp.where(lane < width, first, second)


def fetch(sems, pairs):
    copies = [pltpu.make_async_copy(src, dst, sems.at[i]) for i, (src, dst) in enumerate(pairs)]
    for copy in copies:
        copy.start()
    return copies


def state_kernel(rate_any, skip_any, dt_any, resets_any, b_any, c_any, x_any, *refs, width):
    place_ref = where_am_i()
    pay_refs, tables, scratch = refs[:RING], refs[RING : RING + 8], refs[RING + 8 :]
    start_ref, reach_ref, b_ref, c_ref, row_ref, count_ref, flip_ref, skip_ref = tables
    rate_s, skip_s, dt_s, resets_s, x_s, w_s, bt_s, thr_s, sems = scratch
    blocks, state, channels = start_ref.shape
    wide = channels // RING
    pairs = wide // LANES
    quarters = [place_ref[1] ^ k for k in range(RING)]
    moves = [(dt_any, dt_s), (resets_any, resets_s), (rate_any, rate_s), (skip_any, skip_s), (b_any, b_ref)]
    moves += [(x_any.at[:, pl.ds(pl.multiple_of(q * wide, wide), wide)], x_s.at[k]) for k, q in enumerate(quarters)]
    moves.append((c_any, c_ref))
    copies = fetch(sems, moves)
    for copy in copies[:4]:
        copy.wait()
    scale, cum, count = prep(dt_s[...], rate_s[...], resets_s[...])
    heads = cum.shape[0]
    for b in range(blocks):
        cols = slice(b * SPAN, (b + 1) * SPAN)
        c, n = cum[:, cols], count[:1, cols]
        end, last = c[:, SPAN - 1 :], n[:, SPAN - 1 :]
        w_s[:, cols] = jnp.where(n == last, jnp.exp2(end - c), 0.0) * scale[:, cols]
        through = jnp.where(last == 0.0, jnp.exp2(end), 0.0)
        thr_s[:, b * LANES : (b + 1) * LANES] = jnp.broadcast_to(through, (heads, LANES))
    copies[4].wait()
    bt_s[...] = b_ref[...].astype(F32).T
    two = 4 * pairs
    for k, quarter in enumerate(quarters):
        own = pl.ds(pl.multiple_of(quarter // 2 * two, two), two)
        odd = quarter % 2 == 1

        def rows_of(ref, cols):
            both = ref[own, cols]
            return jnp.where(odd, both[two // 2 :], both[: two // 2])

        copies[5 + k].wait()
        for i in range(pairs):
            lanes = pl.ds(pl.multiple_of(quarter * wide + i * LANES, LANES), LANES)
            running = jnp.zeros((state, LANES), F32)
            product = jnp.ones((1, LANES), F32)
            for b in range(blocks):
                cols = slice(b * SPAN, (b + 1) * SPAN)
                start_ref[b, :, lanes] = running.astype(BF16)
                reach_ref[b, :, lanes] = jnp.broadcast_to(product, (8, LANES))
                x = x_s[k, cols, i * LANES : (i + 1) * LANES]
                rows = rows_of(w_s, cols)
                parts = []
                for j in range(2):
                    left = (bt_s[:, cols] * rows[2 * i + j : 2 * i + j + 1]).astype(BF16)
                    parts.append(jnp.dot(left, x, preferred_element_type=F32))
                fresh = halves(parts[0], parts[1], (state, LANES), width)
                thr = rows_of(thr_s, slice(b * LANES, (b + 1) * LANES))
                thr = halves(thr[2 * i : 2 * i + 1], thr[2 * i + 1 : 2 * i + 2], (1, LANES), width)
                running = thr * running + fresh
                product = product * thr
            pay_refs[k][i, :state, :] = running.astype(BF16)
            pay_refs[k][i, state:, :] = split(product)
    row_ref[...] = cum - jnp.log2(scale)
    count_ref[...] = count
    skip_ref[...] = jnp.broadcast_to(column_of(skip_s[...]), (heads, LANES))
    start = jnp.where(count[:1] == 0.0, jnp.exp2(cum), 0.0)
    for b in range(blocks):
        cols = slice(b * SPAN, (b + 1) * SPAN)
        stack = [cum[:, cols], start[:, cols], count[:, cols], jnp.zeros((LANES - 2 * heads - 8, SPAN), F32)]
        flip_ref[b] = jnp.concatenate(stack, axis=0).T
    copies[5 + RING].wait()


def split(product):
    high = product.astype(BF16).astype(F32)
    mid = (product - high).astype(BF16).astype(F32)
    low = product - high - mid
    row = lax.broadcasted_iota(jnp.int32, (TAIL, LANES), 0)
    tail = jnp.where(row == 0, high, jnp.where(row == 1, mid, jnp.where(row == 2, low, 0.0)))
    return tail.astype(BF16)


def joined(tail):
    tail = tail.astype(F32)
    return tail[0:1] + tail[1:2] + tail[2:3]


VECTORS = pl.BlockSpec(memory_space=pltpu.VMEM)
ANYWHERE = pl.BlockSpec(memory_space=pl.ANY)


def states(dt, rate, skip, resets, bmat, cmat, xs, blocks, width):
    tokens, channels = xs.shape
    heads, state = dt.shape[0], bmat.shape[1]
    wide = channels // RING
    pay = (wide // LANES, state + TAIL, LANES)
    return pl.pallas_call(
        functools.partial(state_kernel, width=width),
        in_specs=[ANYWHERE] * 7,
        out_specs=[VECTORS] * (RING + 8),
        scratch_shapes=[
            pltpu.VMEM((1, heads), F32),
            pltpu.VMEM((1, heads), F32),
            pltpu.VMEM((heads, tokens), jnp.int32),
            pltpu.VMEM((1, tokens), jnp.int32),
            pltpu.VMEM((RING, tokens, wide), BF16),
            pltpu.VMEM((heads, tokens), F32),
            pltpu.VMEM((state, tokens), F32),
            pltpu.VMEM((heads, blocks * LANES), F32),
            pltpu.SemaphoreType.DMA((6 + RING,)),
        ],
        out_shape=[
            *[jax.ShapeDtypeStruct(pay, BF16)] * RING,
            jax.ShapeDtypeStruct((blocks, state, channels), BF16),
            jax.ShapeDtypeStruct((blocks, 8, channels), F32),
            jax.ShapeDtypeStruct((tokens, state), BF16),
            jax.ShapeDtypeStruct((tokens, state), BF16),
            jax.ShapeDtypeStruct((heads, tokens), F32),
            jax.ShapeDtypeStruct((8, tokens), F32),
            jax.ShapeDtypeStruct((blocks, SPAN, LANES), F32),
            jax.ShapeDtypeStruct((heads, LANES), F32),
        ],
        cost_estimate=pl.CostEstimate(flops=4 * tokens * channels * state, bytes_accessed=4 << 20, transcendentals=tokens * heads),
        compiler_params=PARAMS,
        name="states",
    )(rate, skip, dt, resets, bmat, cmat, xs)


def swapped(items, mine):
    a, b, c, d = items
    odd, high = mine % 2 == 1, mine // 2 == 1
    a, b, c, d = jnp.where(odd, b, a), jnp.where(odd, a, b), jnp.where(odd, d, c), jnp.where(odd, c, d)
    return jnp.where(high, c, a), jnp.where(high, d, b), jnp.where(high, a, c), jnp.where(high, b, d)


def prefix_kernel(*refs):
    pays, (total_ref, before_ref, reach_ref) = refs[:RING], refs[RING:]
    pairs, rows, _ = total_ref.shape
    state = rows - TAIL
    mine = where_am_i()[1]
    for i in range(pairs):
        items = swapped([p[i].astype(F32) for p in pays], mine)
        running = jnp.zeros((state, LANES), F32)
        product = jnp.ones((1, LANES), F32)
        before, reach = [], []
        for item in items:
            before.append(running)
            reach.append(jnp.broadcast_to(product, (8, LANES)))
            decay = joined(item[state:])
            running = decay * running + item[:state]
            product = decay * product
        for k, (first, second) in enumerate(zip(swapped(before, mine), swapped(reach, mine))):
            before_ref[k, i] = first
            reach_ref[k, i] = second
        total_ref[i, :state, :] = running.astype(BF16)
        total_ref[i, state:, :] = split(product)


def prefix(pays):
    pairs, rows, _ = pays[0].shape
    return pl.pallas_call(
        prefix_kernel,
        in_specs=[VECTORS] * RING,
        out_shape=[
            jax.ShapeDtypeStruct((pairs, rows, LANES), BF16),
            jax.ShapeDtypeStruct((RING, pairs, rows - TAIL, LANES), F32),
            jax.ShapeDtypeStruct((RING, pairs, 8, LANES), F32),
        ],
        cost_estimate=pl.CostEstimate(flops=1 << 20, bytes_accessed=1 << 19, transcendentals=0),
        compiler_params=PARAMS,
        name="prefix",
    )(*pays)


def spread_kernel(left_ref, before_ref, reach_ref, *outs, always):
    for k, out_ref in enumerate(outs):
        for i in range(out_ref.shape[0]):
            left = left_ref[i, : out_ref.shape[1], :].astype(F32)
            if not always:
                left = jnp.where(where_am_i()[2] % 2 == 1, left, 0.0)
            out_ref[i] = (before_ref[k, i] + reach_ref[k, i, 0:1, :] * left).astype(BF16)


def spread(left, before, reach, always):
    shape = before.shape[1:]
    vmem = pl.BlockSpec(memory_space=pltpu.VMEM)
    return pl.pallas_call(
        functools.partial(spread_kernel, always=always),
        in_specs=[vmem, vmem, vmem],
        out_shape=[jax.ShapeDtypeStruct(shape, BF16)] * RING,
        cost_estimate=pl.CostEstimate(flops=1 << 20, bytes_accessed=1 << 19, transcendentals=0),
        compiler_params=PARAMS,
        name="spread",
    )(left, before, reach)


def across(total, rings):
    state = total.shape[1] - TAIL
    shards = RING * rings
    level, send, gone, reach = 1, total, None, None
    while level < rings:
        got = lax.ppermute(send, "seq", [(i, i ^ (RING * level)) for i in range(shards)])
        if rings == 2:
            return got
        later = (where_am_i()[2] // level) % 2 == 1
        wide = lambda a: (a[:, :state].astype(F32), a[:, state : state + 3].astype(F32).sum(axis=1, keepdims=True))
        (mine, mine_p), (other, other_p) = wide(send), wide(got)
        if gone is None:
            gone, reach = jnp.zeros_like(mine), jnp.ones_like(mine_p)
        gone = jnp.where(later, gone + reach * other, gone)
        reach = jnp.where(later, reach * other_p, reach)
        both = jnp.where(later, mine + mine_p * other, other + other_p * mine)
        tail = (mine_p * other_p).astype(F32)
        high = lax.reduce_precision(tail, 8, 7)
        mid = lax.reduce_precision(tail - high, 8, 7)
        low = tail - high - mid
        rest = jnp.zeros((tail.shape[0], TAIL - 3, LANES), F32)
        send = jnp.concatenate([both, high, mid, low, rest], axis=1).astype(BF16)
        level *= 2
    pad = jnp.zeros((gone.shape[0], TAIL, LANES), F32)
    return jnp.concatenate([gone, pad], axis=1).astype(BF16)


def intra_kernel(skip_ref, b_ref, c_ref, row_ref, count_ref, flip_ref, x_any, g_any, w_any, *refs, k, teams, which, width):
    *outs, x_ref, g_ref, sems = refs
    base_ref, carry_ref = outs[:2]
    block = block_of(where_am_i(), k, teams, which)
    at = pl.ds(pl.multiple_of(block * SPAN, SPAN), SPAN)
    wide = x_ref.shape[1] // RING
    moves = []
    for i in range(RING):
        lanes = slice(i * wide, (i + 1) * wide)
        moves += [(x_any.at[at, lanes], x_ref.at[:, lanes]), (g_any.at[at, lanes], g_ref.at[:, lanes])]
    for out in outs[2:]:
        moves.append((w_any.at[:, : out.shape[1]], out))
    copies = fetch(sems, moves)
    rows, count, flipped = row_ref[:, at], count_ref[:, at], flip_ref[block]
    heads = rows.shape[0]
    dots = lax.dot_general(c_ref[at, :], b_ref[at, :], (((1,), (1,)), ((), ())), preferred_element_type=F32)
    i = lax.broadcasted_iota(jnp.int32, (SPAN, SPAN), 0)
    j = lax.broadcasted_iota(jnp.int32, (SPAN, SPAN), 1)
    linked = (flipped[:, 2 * heads : 2 * heads + 1] == count[:1]) & (j <= i)
    dots = jnp.where(linked, dots, 0.0)
    for pair in range(heads // 2):
        lanes = slice(pair * LANES, (pair + 1) * LANES)
        if pair * LANES % wide == 0:
            for copy in copies[2 * (pair * LANES // wide) :][:2]:
                copy.wait()
        x = x_ref[:, lanes]
        left, right = [], []
        for k in range(2):
            h = 2 * pair + k
            gap = jnp.minimum(flipped[:, h : h + 1] - rows[h : h + 1], 0.0)
            left.append((jnp.exp2(gap) * dots).astype(BF16))
            zero = jnp.zeros_like(x)
            right.append(halves(x, zero, x.shape, width) if k == 0 else halves(zero, x, x.shape, width))
        intra = jnp.dot(jnp.concatenate(left, axis=1), jnp.concatenate(right, axis=0), preferred_element_type=F32)
        weight = halves(skip_ref[2 * pair : 2 * pair + 1], skip_ref[2 * pair + 1 : 2 * pair + 2], (1, LANES), width)
        gate = g_ref[:, lanes].astype(F32)
        gate = gate / (1.0 + jnp.exp(-gate))
        base_ref[:, lanes] = (intra + weight * x.astype(F32)) * gate
        h = heads + 2 * pair
        carry = halves(flipped[:, h : h + 1], flipped[:, h + 1 : h + 2], x.shape, width)
        carry_ref[:, lanes] = (carry * gate).astype(BF16)
    for copy in copies[2 * RING :]:
        copy.wait()


def intra(k, teams, which, tables, xs, gate, weight, columns, width):
    channels = xs.shape[1]
    heads = tables[0].shape[0]
    extra = [jax.ShapeDtypeStruct((weight.shape[0], columns), BF16)] if columns else []
    return pl.pallas_call(
        functools.partial(intra_kernel, k=k, teams=teams, which=which, width=width),
        in_specs=[VECTORS] * 6 + [ANYWHERE] * 3,
        out_specs=[VECTORS] * (2 + len(extra)),
        scratch_shapes=[
            pltpu.VMEM((SPAN, channels), BF16),
            pltpu.VMEM((SPAN, channels), BF16),
            pltpu.SemaphoreType.DMA((2 * RING + len(extra),)),
        ],
        out_shape=[jax.ShapeDtypeStruct((SPAN, channels), F32), jax.ShapeDtypeStruct((SPAN, channels), BF16), *extra],
        cost_estimate=pl.CostEstimate(
            flops=8 * SPAN * SPAN * channels, bytes_accessed=2 << 20, transcendentals=heads * SPAN * SPAN
        ),
        compiler_params=PARAMS,
        name="intra",
    )(*tables, xs, gate, weight)


def finish_kernel(base_ref, carry_ref, c_ref, start_ref, reach_ref, gain_ref, *refs, k, teams, which):
    place_ref = where_am_i()
    in_refs, (hid_ref, sq_ref) = refs[:RING], refs[RING:]
    block = block_of(place_ref, k, teams, which)
    query = c_ref[pl.ds(pl.multiple_of(block * SPAN, SPAN), SPAN), :]
    pairs = in_refs[0].shape[0]
    wide = pairs * LANES
    total = jnp.zeros((SPAN, LANES), F32)
    quarters = [jnp.concatenate([r[i] for i in range(pairs)], axis=1).astype(F32) for r in in_refs]
    for q, incoming in enumerate(swapped(quarters, place_ref[1])):
        lanes = slice(q * wide, (q + 1) * wide)
        full = start_ref[block, :, lanes].astype(F32) + reach_ref[block, 0:1, lanes] * incoming
        inter = jnp.dot(query, full.astype(BF16), preferred_element_type=F32)
        gated = base_ref[:, lanes] + carry_ref[:, lanes].astype(F32) * inter
        square = gated * gated
        for i in range(pairs):
            total = total + square[:, i * LANES : (i + 1) * LANES]
        hid_ref[:, lanes] = (gated * gain_ref[0:1, lanes]).astype(BF16)
    sums = jnp.sum(total.T, axis=0, keepdims=True)
    sq_ref[...] = jnp.broadcast_to(sums, (8, SPAN))


def finish(k, teams, which, locals_, cmat, starts, reach, gain, incoming):
    channels = gain.shape[1]
    state = incoming[0].shape[1]
    return pl.pallas_call(
        functools.partial(finish_kernel, k=k, teams=teams, which=which),
        in_specs=[VECTORS] * (6 + RING),
        out_specs=[VECTORS] * 2,
        out_shape=[
            jax.ShapeDtypeStruct((SPAN, channels), BF16),
            jax.ShapeDtypeStruct((8, SPAN), F32),
        ],
        cost_estimate=pl.CostEstimate(flops=2 * SPAN * state * channels, bytes_accessed=3 << 20, transcendentals=0),
        compiler_params=PARAMS,
        name="finish",
    )(*locals_, cmat, starts, reach, gain, *incoming)


def product_kernel(*refs, count):
    wa, wb = refs[2 * count][...], refs[2 * count + 1][...]
    for i in range(count):
        total = jnp.dot(refs[2 * i][...], wa, preferred_element_type=F32)
        total = total + jnp.dot(refs[2 * i + 1][...], wb, preferred_element_type=F32)
        out_ref = refs[2 * count + 2 + i]
        out_ref[...] = total.astype(out_ref.dtype)


def product(lefts, dtypes, wa, wb, first, columns, tile):
    rows, depth = lefts[0][0].shape
    count = len(lefts)
    left = pl.BlockSpec((rows, depth), lambda i: (0, 0))
    right = pl.BlockSpec((depth, tile), lambda i: (0, first // tile + i))
    return pl.pallas_call(
        functools.partial(product_kernel, count=count),
        grid=(columns // tile,),
        in_specs=[left, left] * count + [right, right],
        out_specs=[pl.BlockSpec((rows, tile), lambda i: (0, i))] * count,
        out_shape=[jax.ShapeDtypeStruct((rows, columns), dtype) for dtype in dtypes],
        cost_estimate=pl.CostEstimate(
            flops=4 * count * rows * depth * columns, bytes_accessed=4 * depth * columns, transcendentals=0
        ),
        compiler_params=PARAMS,
        name="product",
    )(*(a for pair in lefts for a in pair), wa, wb)


def first_kernel(a_ref, b_ref, wa_ref, wb_any, out_ref, w_s, sems, *, step):
    depth, columns = w_s.shape
    parts = [slice(i, i + step) for i in range(0, depth, step)]
    copies = fetch(sems, [(wb_any.at[part, :columns], w_s.at[part]) for part in parts])
    total = jnp.dot(a_ref[...], wa_ref[...], preferred_element_type=F32)
    for copy, part in zip(copies, parts):
        copy.wait()
        total = total + jnp.dot(b_ref[:, part], w_s[part], preferred_element_type=F32)
    out_ref[...] = total.astype(out_ref.dtype)


def first_product(a, b, wa, wb, step=512):
    rows, depth = a.shape
    columns = wa.shape[1]
    return pl.pallas_call(
        functools.partial(first_kernel, step=step),
        in_specs=[VECTORS] * 3 + [ANYWHERE],
        out_specs=VECTORS,
        out_shape=jax.ShapeDtypeStruct((rows, columns), BF16),
        scratch_shapes=[pltpu.VMEM((depth, columns), BF16), pltpu.SemaphoreType.DMA((depth // step,))],
        cost_estimate=pl.CostEstimate(flops=4 * rows * depth * columns, bytes_accessed=4 * depth * columns, transcendentals=0),
        compiler_params=PARAMS,
        name="first",
    )(a, b, wa, wb)


def close(square, own, parts, inner, out, first, columns, shape, step=256):
    rows = shape[0]

    def body(*refs):
        sq_ref, own_ref = refs[:2]
        part_refs = refs[2 : 2 + len(parts)]
        out_any, made_s, sems = refs[-3:]
        row = lax.rsqrt(sq_ref[...] / inner + 1e-05).T[:, 0:1]
        copies = []
        for i in range(columns // step):
            here = slice(i * step, (i + 1) * step)
            total = own_ref[:, here]
            for part in part_refs:
                total = total + part[:, here].astype(F32)
            made_s[:, here] = (total * row).astype(BF16)
            there = slice(first + i * step, first + (i + 1) * step)
            copies.append(pltpu.make_async_copy(made_s.at[:, here], out_any.at[:, there], sems.at[i]))
            copies[-1].start()
        for copy in copies:
            copy.wait()

    args = [square, own, *parts]
    in_specs = [VECTORS] * len(args)
    aliases = {}
    if out is not None:
        in_specs.append(ANYWHERE)
        args.append(out)
        aliases = {len(args) - 1: 0}
    return pl.pallas_call(
        body,
        in_specs=in_specs,
        out_specs=ANYWHERE,
        out_shape=jax.ShapeDtypeStruct(shape, BF16),
        scratch_shapes=[pltpu.VMEM((rows, columns), BF16), pltpu.SemaphoreType.DMA((columns // step,))],
        input_output_aliases=aliases,
        cost_estimate=pl.CostEstimate(flops=4 * rows * columns, bytes_accessed=8 * rows * columns, transcendentals=0),
        compiler_params=PARAMS,
        name="close",
    )(*args)


def local(xs, gate, bmat, cmat, dt, resets, decay_rate, skip, gain, weight, *, shards, group):
    tokens, channels = xs.shape
    heads = dt.shape[0]
    width = channels // heads
    blocks = tokens // SPAN
    inner = float(group * channels)
    out_columns = weight.shape[1]
    teams = group // 2
    rings = shards // RING

    swap = [(i, i ^ 1) for i in range(group)]
    unit = out_columns // sum(CUTS)
    raw = weight
    held = (xs, gate, bmat, cmat, dt, weight, decay_rate[None, :], skip[None, :], resets[None, :])
    held = [pltpu.with_memory_space_constraint(a, pltpu.HBM) for a in held]
    xs, gate, bmat, cmat, dt, weight, decay_rate, skip, flags = held
    gains = gain[None, :]

    def after(value, *others):
        return lax.optimization_barrier((value, *others))[0]

    def inside(k, which, when):
        columns = CUTS[0] * unit if (k, which) == (0, 1) else 0
        return intra(k, teams, which, (when, *tables), xs, gate, weight, columns, width)

    def around(items):
        got = [items[0]]
        for k in range(1, RING):
            got.append(lax.ppermute(items[k], "seq", [(i, i ^ k) for i in range(shards)]))
        return got

    *pays, starts, reach, keys, queries, row, count, flip, direct = states(
        dt, decay_rate, skip, flags, bmat, cmat, xs, blocks, width
    )
    tables = (keys, queries, row, count, flip)
    weight_b = lax.ppermute(after(raw, pays[0]), "head", swap)
    gathered = around(pays)
    locals_ = {}
    early = after(direct, pays[0])
    for k in range(1, teams):
        locals_[k, 1] = inside(k, 1, early)
    total, before, ahead = prefix(gathered)
    left = across(total, rings)
    early = after(direct, total)
    for k in range(1, teams):
        locals_[k, 0] = inside(k, 0, early)
    outgoing = spread(left, before, ahead, rings > 2)
    incoming = around(outgoing)
    *locals_[0, 1], ready = inside(0, 1, after(direct, outgoing[0]))

    def pair_of(k, when):
        done = []
        late = after(gains, when)
        for which in (1, 0):
            if (k, which) not in locals_:
                locals_[k, which] = inside(k, which, when)
            hidden, sq = finish(k, teams, which, locals_[k, which], queries, starts, reach, late, incoming)
            done.append((hidden, sq))
        other = lax.ppermute(done[0][0], "head", swap)
        square = done[1][1] + lax.ppermute(done[0][1], "head", swap)
        return done[1][0], other, square

    places = [sum(CUTS[:c]) * unit for c in range(len(CUTS) + 1)]
    received = [[] for _ in CUTS]
    squares = []
    owns = {}
    mine, last = None, direct
    for k in range(1, teams):
        hidden, other, square = pair_of(k, last)
        send = [(i, (i + 2 * k) % group) for i in range(group)]
        squares.append(lax.ppermute(square, "head", send))
        for c, n in enumerate(CUTS):
            if c == ALONE and mine is None:
                *mine, square = pair_of(0, last)
                squares.append(square)
            both = c >= ALONE and k == 1
            if c == 0:
                made = [first_product(hidden, other, ready, weight_b)]
            else:
                made = product(
                    [(hidden, other), mine] if both else [(hidden, other)],
                    [BF16, F32] if both else [BF16],
                    weight,
                    weight_b,
                    places[c],
                    n * unit,
                    unit,
                )
            hidden, made = lax.optimization_barrier((hidden, made))
            if both:
                owns[c] = made[1]
            received[c].append(lax.ppermute(made[0], "head", send))
            last = after(direct, made[0])
    mine, _ = lax.optimization_barrier((mine, made[0]))
    early = product([mine], [F32], weight, weight_b, 0, places[ALONE], places[ALONE] // 3)[0]
    square = sum(squares[1:], squares[0])
    out = None
    for c, n in enumerate(CUTS):
        own = early[:, places[c] : places[c + 1]] if c < ALONE else owns[c]
        out = close(square, own, received[c], inner, out, places[c], n * unit, (SPAN, out_columns))
        if c + 1 < len(CUTS):
            out, received[c + 1] = lax.optimization_barrier((out, received[c + 1]))
    return out


def solution(mesh):
    in_specs = (
        P("seq", "head"),
        P("seq", "head"),
        P("seq", None),
        P("seq", None),
        P("head", "seq"),
        P("seq"),
        P("head"),
        P("head"),
        P("head"),
        P("head", None),
    )
    out_specs = P(("seq", "head"), None)
    body = functools.partial(local, shards=mesh.shape["seq"], group=mesh.shape["head"])

    return jax.shard_map(body, mesh=mesh, in_specs=in_specs, out_specs=out_specs, check_vma=False)
```

profile of v0, /device:TPU:0, one launch (start us, length us, event | category | flops | bytes accessed | tf_op | source)
XLA Modules:
  0.0 95.0 jit_solution(15967109616813973463)
XLA Ops:
  0.0 3.6 %states.1 = (bf16[2,136,128]{2,1,0:T(8,128)(2,1)S(1)}, bf16[2,136,128]{2,1,0:T(8,128)(2,1)S(1)}, bf16[2,136,128]{2,1,0:T(8,128)(2,1)S(1)}, bf16[2,136,128]{2,1,0...) custom-call(f32[1,16]{1,0:T(1,128)} %bitcast.9, ...), custom_call_target="tpu_custom_call" | custom-call | flops 536870912 | bytes 4194304 | tf_op jit(solution)/shard_map/states/pallas_call | solution.py:161
  3.6 0.5 collective-permute-start.10
  4.1 2.6 %collective-permute-start = (bf16[2,136,128]{2,1,0:T(8,128)(2,1)S(1)}, bf16[2,136,128]{2,1,0:T(8,128)(2,1)S(1)}, u32[]{:S(2)}, u32[]{:S(2)}) collective-permute-start(bf16[2,136,128]{2,1,0:T(8,128)(2,1)S(1)} %get-tuple-element.82), channel_id=1, source_target_pairs={{0,4},{4,0},{8,12},{12,8},{16,20},{20,16},{24,28},{28,24},{1,5},{5... | collective-permute-start | bytes 208904 | tf_op jit(solution)/shard_map/ppermute | solution.py:517
  6.7 1.6 %collective-permute-start.1 = (bf16[2,136,128]{2,1,0:T(8,128)(2,1)S(1)}, bf16[2,136,128]{2,1,0:T(8,128)(2,1)S(1)}, u32[]{:S(2)}, u32[]{:S(2)}) collective-permute-start(bf16[2,136,128]{2,1,0:T(8,128)(2,1)S(1)} %get-tuple-element.83), channel_id=1, source_target_pairs={{0,8},{4,12},{8,0},{12,4},{16,24},{20,28},{24,16},{28,20},{1,9},{5... | collective-permute-start | bytes 208904 | tf_op jit(solution)/shard_map/ppermute | solution.py:517
  8.3 1.2 %collective-permute-done.refs_1_ = bf16[2,136,128]{2,1,0:T(8,128)(2,1)S(1)} collective-permute-done((bf16[2,136,128]{2,1,0:T(8,128)(2,1)S(1)}, bf16[2,136,128]{2,1,0:T(8,128)(2,1)S(1)}, u32[]{:S(2)}, u32[]{:S(2)}) %collective-permute-start) | collective-permute-done | bytes 69664 | tf_op jit(solution)/shard_map/ppermute | solution.py:517
  9.5 1.8 %collective-permute-done.1.refs_2_ = bf16[2,136,128]{2,1,0:T(8,128)(2,1)S(1)} collective-permute-done((bf16[2,136,128]{2,1,0:T(8,128)(2,1)S(1)}, bf16[2,136,128]{2,1,0:T(8,128)(2,1)S(1)}, u32[]{:S(2)}, u32[]{:S(2)}) %collective-permute-start.1) | collective-permute-done | bytes 69664 | tf_op jit(solution)/shard_map/ppermute | solution.py:517
  11.3 2.2 %collective-permute-done.2.refs_3_ = bf16[2,136,128]{2,1,0:T(8,128)(2,1)S(1)} collective-permute-done((bf16[2,136,128]{2,1,0:T(8,128)(2,1)S(1)}, bf16[2,136,128]{2,1,0:T(8,128)(2,1)S(1)}, u32[]{:S(2)}, u32[]{:S(2)}) %collective-permute-start.2) | collective-permute-done | bytes 69664 | tf_op jit(solution)/shard_map/ppermute | solution.py:517
  13.5 0.2 prefix.1
  13.7 2.6 %collective-permute-start.3 = (bf16[2,136,128]{2,1,0:T(8,128)(2,1)S(1)}, bf16[2,136,128]{2,1,0:T(8,128)(2,1)S(1)}, u32[]{:S(2)}, u32[]{:S(2)}) collective-permute-start(bf16[2,136,128]{2,1,0:T(8,128)(2,1)S(1)} %get-tuple-element.85), channel_id=1, source_target_pairs={{0,16},{4,20},{8,24},{12,28},{16,0},{20,4},{24,8},{28,12},{1,17},{... | collective-permute-start | bytes 208904 | tf_op jit(solution)/shard_map/ppermute | solution.py:266
  16.3 3.4 %collective-permute-done.3.left_ref = bf16[2,136,128]{2,1,0:T(8,128)(2,1)S(1)} collective-permute-done((bf16[2,136,128]{2,1,0:T(8,128)(2,1)S(1)}, bf16[2,136,128]{2,1,0:T(8,128)(2,1)S(1)}, u32[]{:S(2)}, u32[]{:S(2)}) %collective-permute-start.3) | collective-permute-done | bytes 69664 | tf_op jit(solution)/shard_map/ppermute | solution.py:266
  19.8 1.2 %collective-permute-start.5 = (bf16[2,128,128]{2,1,0:T(8,128)(2,1)S(1)}, bf16[2,128,128]{2,1,0:T(8,128)(2,1)S(1)}, u32[]{:S(2)}, u32[]{:S(2)}) collective-permute-start(bf16[2,128,128]{2,1,0:T(8,128)(2,1)S(1)} %get-tuple-element.101), channel_id=1, source_target_pairs={{0,8},{4,12},{8,0},{12,4},{16,24},{20,28},{24,16},{28,20},{1,9},{5... | collective-permute-start | bytes 196616 | tf_op jit(solution)/shard_map/ppermute | solution.py:517
  21.1 2.2 %collective-permute-start.6 = (bf16[2,128,128]{2,1,0:T(8,128)(2,1)S(1)}, bf16[2,128,128]{2,1,0:T(8,128)(2,1)S(1)}, u32[]{:S(2)}, u32[]{:S(2)}) collective-permute-start(bf16[2,128,128]{2,1,0:T(8,128)(2,1)S(1)} %get-tuple-element.102), channel_id=1, source_target_pairs={{0,12},{4,8},{8,4},{12,0},{16,28},{20,24},{24,20},{28,16},{1,13},{... | collective-permute-start | bytes 196616 | tf_op jit(solution)/shard_map/ppermute | solution.py:517
  23.3 2.9 %intra.5 = (f32[256,1024]{1,0:T(8,128)S(1)}, bf16[256,1024]{1,0:T(8,128)(2,1)S(1)}) custom-call(f32[16,128]{1,0:T(8,128)S(1)} %get-tuple-element.116.skip_ref, bf16[1024,128]{1,0:T(8,128)(2,1)S(1)} %get-tuple-element.87.b_ref, bf16[1024,128]{1,0:T(8,128)(2,1)S(1)} %get-tuple-element.88.c_ref, f32[16,1024]{1,0:T(8,128)S(1)} %get-tuple-element.89.row_ref, ...), custom_call_target="tpu_custom_call" | custom-call | flops 536870912 | bytes 2097152 | tf_op jit(solution)/shard_map/intra/pallas_call | solution.py:337
  26.3 0.6 finish.5
  26.9 2.9 %intra.4 = (f32[256,1024]{1,0:T(8,128)S(1)}, bf16[256,1024]{1,0:T(8,128)(2,1)S(1)}) custom-call(f32[16,128]{1,0:T(8,128)S(1)} %get-tuple-element.116.skip_ref, bf16[1024,128]{1,0:T(8,128)(2,1)S(1)} %get-tuple-element.87.b_ref, bf16[1024,128]{1,0:T(8,128)(2,1)S(1)} %get-tuple-element.88.c_ref, f32[16,1024]{1,0:T(8,128)S(1)} %get-tuple-element.89.row_ref, ...), custom_call_target="tpu_custom_call" | custom-call | flops 536870912 | bytes 2097152 | tf_op jit(solution)/shard_map/intra/pallas_call | solution.py:337
  29.9 3.0 %intra.6 = (f32[256,1024]{1,0:T(8,128)S(1)}, bf16[256,1024]{1,0:T(8,128)(2,1)S(1)}, bf16[1024,256]{1,0:T(8,128)(2,1)S(1)}) custom-call(f32[16,128]{1,0:T(8,128)S(1)} %get-tuple-element.116.skip_ref, bf16[1024,128]{1,0:T(8,128)(2,1)S(1)} %get-tuple-element.87.b_ref, bf16[1024,128]{1,0:T(8,128)(2,1)S(1)} %get-tuple-element.88.c_ref, ...), custom_call_target="tpu_custom_call" | custom-call | flops 536870912 | bytes 2097152 | tf_op jit(solution)/shard_map/intra/pallas_call | solution.py:337
  32.8 0.6 finish.4
  33.4 1.1 %first.1 = bf16[256,256]{1,0:T(8,128)(2,1)S(1)} custom-call(bf16[256,1024]{1,0:T(8,128)(2,1)S(1)} %get-tuple-element.132.a_ref.refs_0_, bf16[256,1024]{1,0:T(8,128)(2,1)S(1)} %collective-permute-done.9.b_ref.refs_1_, bf16[1024,256]{1,0:T(8,128)(2,1)S(1)} %get-tuple-element.111.wa_ref, bf16[1024,4096]{1,0:T(8,128)(2,1)S(1)} %collective-permute-done.10.wb_any.refs_3_.refs_5_), custom_call_target="tpu_custom_call" | custom-call | flops 268435456 | bytes 1048576 | tf_op jit(solution)/shard_map/first/pallas_call | solution.py:436
  34.5 3.0 %product.6 = bf16[256,768]{1,0:T(8,128)(2,1)S(1)} custom-call(bf16[256,1024]{1,0:T(8,128)(2,1)S(1)} %get-tuple-element.132.a_ref.refs_0_, bf16[256,1024]{1,0:T(8,128)(2,1)S(1)} %collective-permute-done.9.b_ref.refs_1_, bf16[1024,4096]{1,0:T(8,128)(2,1)} %refs_2_.5, bf16[1024,4096]{1,0:T(8,128)(2,1)S(1)} %collective-permute-done.10.wb_any.refs_3_.refs_5_), custom_call_target="tpu_custom_call" | custom-call | flops 805306368 | bytes 3145728 | tf_op jit(solution)/shard_map/product/pallas_call | solution.py:408
  37.5 4.6 %product.7 = bf16[256,1280]{1,0:T(8,128)(2,1)S(1)} custom-call(bf16[256,1024]{1,0:T(8,128)(2,1)S(1)} %get-tuple-element.132.a_ref.refs_0_, bf16[256,1024]{1,0:T(8,128)(2,1)S(1)} %collective-permute-done.9.b_ref.refs_1_, bf16[1024,4096]{1,0:T(8,128)(2,1)} %refs_2_.5, bf16[1024,4096]{1,0:T(8,128)(2,1)S(1)} %collective-permute-done.10.wb_any.refs_3_.refs_5_), custom_call_target="tpu_custom_call" | custom-call | flops 1342177280 | bytes 5242880 | tf_op jit(solution)/shard_map/product/pallas_call | solution.py:408
  42.1 0.6 finish.7
  42.7 0.5 collective-permute-start.12
  43.3 1.5 %collective-permute-done.7 = f32[8,256]{1,0:T(8,128)S(1)} collective-permute-done((f32[8,256]{1,0:T(8,128)S(1)}, f32[8,256]{1,0:T(8,128)S(1)}, u32[]{:S(2)}, u32[]{:S(2)}) %collective-permute-start.7) | collective-permute-done | bytes 8224 | tf_op jit(solution)/shard_map/ppermute | solution.py:548
  44.8 1.5 %collective-permute-start.8 = (f32[8,256]{1,0:T(8,128)S(1)}, f32[8,256]{1,0:T(8,128)S(1)}, u32[]{:S(2)}, u32[]{:S(2)}) collective-permute-start(f32[8,256]{1,0:T(8,128)S(1)} %add.9), channel_id=1, source_target_pairs={{0,2},{1,3},{2,0},{3,1},{4,6},{5,7},{6,4},{7,5},{8,10},{9,11},{10,... | collective-permute-start | bytes 24584 | tf_op jit(solution)/shard_map/ppermute | solution.py:559
  46.3 0.5 collective-permute-start.15
  46.8 1.5 %collective-permute-start.13 = (bf16[256,256]{1,0:T(8,128)(2,1)S(1)}, bf16[256,256]{1,0:T(8,128)(2,1)S(1)}, u32[]{:S(2)}, u32[]{:S(2)}) collective-permute-start(bf16[256,256]{1,0:T(8,128)(2,1)S(1)} %first.1), channel_id=1, source_target_pairs={{0,2},{1,3},{2,0},{3,1},{4,6},{5,7},{6,4},{7,5},{8,10},{9,11},{10,... | collective-permute-start | bytes 393224 | tf_op jit(solution)/shard_map/ppermute | solution.py:580
  48.3 0.5 collective-permute-start.14
  48.8 2.9 %intra.7 = (f32[256,1024]{1,0:T(8,128)S(1)}, bf16[256,1024]{1,0:T(8,128)(2,1)S(1)}) custom-call(f32[16,128]{1,0:T(8,128)S(1)} %get-tuple-element.116.skip_ref, bf16[1024,128]{1,0:T(8,128)(2,1)S(1)} %get-tuple-element.87.b_ref, bf16[1024,128]{1,0:T(8,128)(2,1)S(1)} %get-tuple-element.88.c_ref, f32[16,1024]{1,0:T(8,128)S(1)} %get-tuple-element.89.row_ref, ...), custom_call_target="tpu_custom_call" | custom-call | flops 536870912 | bytes 2097152 | tf_op jit(solution)/shard_map/intra/pallas_call | solution.py:337
  51.7 0.6 finish.6
  52.4 3.6 %product.8 = (bf16[256,768]{1,0:T(8,128)(2,1)S(1)}, f32[256,768]{1,0:T(8,128)S(1)}) custom-call(bf16[256,1024]{1,0:T(8,128)(2,1)S(1)} %get-tuple-element.132.a_ref.refs_0_, bf16[256,1024]{1,0:T(8,128)(2,1)S(1)} %collective-permute-done.9.b_ref.refs_1_, bf16[256,1024]{1,0:T(8,128)(2,1)S(1)} %get-tuple-element.139.refs_2_.refs_0_, ...), custom_call_target="tpu_custom_call" | custom-call | flops 1610612736 | bytes 3145728 | tf_op jit(solution)/shard_map/product/pallas_call | solution.py:408
  56.1 3.6 %product.9 = (bf16[256,768]{1,0:T(8,128)(2,1)S(1)}, f32[256,768]{1,0:T(8,128)S(1)}) custom-call(bf16[256,1024]{1,0:T(8,128)(2,1)S(1)} %get-tuple-element.132.a_ref.refs_0_, bf16[256,1024]{1,0:T(8,128)(2,1)S(1)} %collective-permute-done.9.b_ref.refs_1_, bf16[256,1024]{1,0:T(8,128)(2,1)S(1)} %get-tuple-element.139.refs_2_.refs_0_, ...), custom_call_target="tpu_custom_call" | custom-call | flops 1610612736 | bytes 3145728 | tf_op jit(solution)/shard_map/product/pallas_call | solution.py:408
  59.7 1.6 %collective-permute-start.16 = (bf16[256,768]{1,0:T(8,128)(2,1)S(1)}, bf16[256,768]{1,0:T(8,128)(2,1)S(1)}, u32[]{:S(2)}, u32[]{:S(2)}) collective-permute-start(bf16[256,768]{1,0:T(8,128)(2,1)S(1)} %get-tuple-element.147), channel_id=1, source_target_pairs={{0,2},{1,3},{2,0},{3,1},{4,6},{5,7},{6,4},{7,5},{8,10},{9,11},{10,... | collective-permute-start | bytes 1179656 | tf_op jit(solution)/shard_map/ppermute | solution.py:580
  61.3 0.5 collective-permute-start.17
  61.8 1.8 %product.10 = (bf16[256,256]{1,0:T(8,128)(2,1)S(1)}, f32[256,256]{1,0:T(8,128)S(1)}) custom-call(bf16[256,1024]{1,0:T(8,128)(2,1)S(1)} %get-tuple-element.132.a_ref.refs_0_, bf16[256,1024]{1,0:T(8,128)(2,1)S(1)} %collective-permute-done.9.b_ref.refs_1_, bf16[256,1024]{1,0:T(8,128)(2,1)S(1)} %get-tuple-element.139.refs_2_.refs_0_, ...), custom_call_target="tpu_custom_call" | custom-call | flops 536870912 | bytes 1048576 | tf_op jit(solution)/shard_map/product/pallas_call | solution.py:408
  63.6 3.1 %collective-permute-done.13.refs_2_ = bf16[256,256]{1,0:T(8,128)(2,1)S(1)} collective-permute-done((bf16[256,256]{1,0:T(8,128)(2,1)S(1)}, bf16[256,256]{1,0:T(8,128)(2,1)S(1)}, u32[]{:S(2)}, u32[]{:S(2)}) %collective-permute-start.13) | collective-permute-done | bytes 131104 | tf_op jit(solution)/shard_map/ppermute | solution.py:580
  66.7 0.5 collective-permute-start.18
  67.2 4.9 %product.11 = f32[256,2304]{1,0:T(8,128)S(1)} custom-call(bf16[256,1024]{1,0:T(8,128)(2,1)S(1)} %get-tuple-element.139.refs_2_.refs_0_, bf16[256,1024]{1,0:T(8,128)(2,1)S(1)} %collective-permute-done.12.refs_3_.refs_1_, bf16[1024,4096]{1,0:T(8,128)(2,1)} %refs_2_.5, bf16[1024,4096]{1,0:T(8,128)(2,1)S(1)} %collective-permute-done.10.wb_any.refs_3_.refs_5_), custom_call_target="tpu_custom_call" | custom-call | flops 2415919104 | bytes 9437184 | tf_op jit(solution)/shard_map/product/pallas_call | solution.py:408
  72.1 0.9 close.6.refs_3_
  73.1 0.1 slice.12.refs_1_
  73.2 1.9 %collective-permute-done.14.refs_2_ = bf16[256,768]{1,0:T(8,128)(2,1)S(1)} collective-permute-done((bf16[256,768]{1,0:T(8,128)(2,1)S(1)}, bf16[256,768]{1,0:T(8,128)(2,1)S(1)}, u32[]{:S(2)}, u32[]{:S(2)}) %collective-permute-start.14) | collective-permute-done | bytes 393248 | tf_op jit(solution)/shard_map/ppermute | solution.py:580
  75.1 1.0 %close.7.refs_3_ = bf16[256,4096]{1,0:T(8,128)(2,1)} custom-call(f32[8,256]{1,0:T(8,128)S(1)} %add_add_fusion.refs_0_, f32[256,768]{1,0:T(8,128)S(1)} %slice.13.refs_1_, bf16[256,768]{1,0:T(8,128)(2,1)S(1)} %collective-permute-done.14.refs_2_, bf16[256,4096]{1,0:T(8,128)(2,1)} %close.6.refs_3_), custom_call_target="tpu_custom_call", output_to_operand_aliasing={{}: (3, {})} | custom-call | flops 786432 | bytes 1572864 | tf_op jit(solution)/shard_map/close/pallas_call | solution.py:476
  76.2 1.2 %close.8.refs_3_ = bf16[256,4096]{1,0:T(8,128)(2,1)} custom-call(f32[8,256]{1,0:T(8,128)S(1)} %add_add_fusion.refs_0_, f32[256,1280]{1,0:T(8,128)S(1)} %slice.12.refs_1_, bf16[256,1280]{1,0:T(8,128)(2,1)S(1)} %collective-permute-done.15.refs_2_, bf16[256,4096]{1,0:T(8,128)(2,1)} %close.7.refs_3_), custom_call_target="tpu_custom_call", output_to_operand_aliasing={{}: (3, {})} | custom-call | flops 1310720 | bytes 2621440 | tf_op jit(solution)/shard_map/close/pallas_call | solution.py:476
  77.4 6.2 %collective-permute-done.16.refs_2_ = bf16[256,768]{1,0:T(8,128)(2,1)S(1)} collective-permute-done((bf16[256,768]{1,0:T(8,128)(2,1)S(1)}, bf16[256,768]{1,0:T(8,128)(2,1)S(1)}, u32[]{:S(2)}, u32[]{:S(2)}) %collective-permute-start.16) | collective-permute-done | bytes 393248 | tf_op jit(solution)/shard_map/ppermute | solution.py:580
  83.5 1.0 %close.9.refs_3_ = bf16[256,4096]{1,0:T(8,128)(2,1)} custom-call(f32[8,256]{1,0:T(8,128)S(1)} %add_add_fusion.refs_0_, f32[256,768]{1,0:T(8,128)S(1)} %get-tuple-element.137.refs_1_, bf16[256,768]{1,0:T(8,128)(2,1)S(1)} %collective-permute-done.16.refs_2_, bf16[256,4096]{1,0:T(8,128)(2,1)} %close.8.refs_3_), custom_call_target="tpu_custom_call", output_to_operand_aliasing={{}: (3, {})} | custom-call | flops 786432 | bytes 1572864 | tf_op jit(solution)/shard_map/close/pallas_call | solution.py:476
  84.6 7.4 %collective-permute-done.17.refs_2_ = bf16[256,768]{1,0:T(8,128)(2,1)S(1)} collective-permute-done((bf16[256,768]{1,0:T(8,128)(2,1)S(1)}, bf16[256,768]{1,0:T(8,128)(2,1)S(1)}, u32[]{:S(2)}, u32[]{:S(2)}) %collective-permute-start.17) | collective-permute-done | bytes 393248 | tf_op jit(solution)/shard_map/ppermute | solution.py:580
  92.0 1.0 %close.10.refs_3_ = bf16[256,4096]{1,0:T(8,128)(2,1)} custom-call(f32[8,256]{1,0:T(8,128)S(1)} %add_add_fusion.refs_0_, f32[256,768]{1,0:T(8,128)S(1)} %get-tuple-element.136.refs_1_, bf16[256,768]{1,0:T(8,128)(2,1)S(1)} %collective-permute-done.17.refs_2_, bf16[256,4096]{1,0:T(8,128)(2,1)} %close.9.refs_3_), custom_call_target="tpu_custom_call", output_to_operand_aliasing={{}: (3, {})} | custom-call | flops 786432 | bytes 1572864 | tf_op jit(solution)/shard_map/close/pallas_call | solution.py:476
  93.0 0.9 collective-permute-done.18.refs_2_
  93.9 0.9 close.11
  (21 shorter events, 0.5 us)
Async XLA Ops:
  3.6 29.8 %collective-permute-start.10 = (bf16[1024,4096]{1,0:T(8,128)(2,1)}, bf16[1024,4096]{1,0:T(8,128)(2,1)S(1)}, u32[]{:S(2)}, u32[]{:S(2)}) collective-permute-start(bf16[1024,4096]{1,0:T(8,128)(2,1)} %refs_2_.5), channel_id=1, source_target_pairs={{0,1},{1,0},{2,3},{3,2},{4,5},{5,4},{6,7},{7,6},{8,9},{9,8},{10,11... | collective-permute-start | bytes 25165832 | tf_op jit(solution)/shard_map/ppermute | solution.py:524
  4.1 5.3 %collective-permute-start = (bf16[2,136,128]{2,1,0:T(8,128)(2,1)S(1)}, bf16[2,136,128]{2,1,0:T(8,128)(2,1)S(1)}, u32[]{:S(2)}, u32[]{:S(2)}) collective-permute-start(bf16[2,136,128]{2,1,0:T(8,128)(2,1)S(1)} %get-tuple-element.82), channel_id=1, source_target_pairs={{0,4},{4,0},{8,12},{12,8},{16,20},{20,16},{24,28},{28,24},{1,5},{5... | collective-permute-start | bytes 208904 | tf_op jit(solution)/shard_map/ppermute | solution.py:517
  6.7 4.6 %collective-permute-start.1 = (bf16[2,136,128]{2,1,0:T(8,128)(2,1)S(1)}, bf16[2,136,128]{2,1,0:T(8,128)(2,1)S(1)}, u32[]{:S(2)}, u32[]{:S(2)}) collective-permute-start(bf16[2,136,128]{2,1,0:T(8,128)(2,1)S(1)} %get-tuple-element.83), channel_id=1, source_target_pairs={{0,8},{4,12},{8,0},{12,4},{16,24},{20,28},{24,16},{28,20},{1,9},{5... | collective-permute-start | bytes 208904 | tf_op jit(solution)/shard_map/ppermute | solution.py:517
  8.3 5.2 %collective-permute-start.2 = (bf16[2,136,128]{2,1,0:T(8,128)(2,1)S(1)}, bf16[2,136,128]{2,1,0:T(8,128)(2,1)S(1)}, u32[]{:S(2)}, u32[]{:S(2)}) collective-permute-start(bf16[2,136,128]{2,1,0:T(8,128)(2,1)S(1)} %get-tuple-element.84), channel_id=1, source_target_pairs={{0,12},{4,8},{8,4},{12,0},{16,28},{20,24},{24,20},{28,16},{1,13},{... | collective-permute-start | bytes 208904 | tf_op jit(solution)/shard_map/ppermute | solution.py:517
  13.7 6.0 %collective-permute-start.3 = (bf16[2,136,128]{2,1,0:T(8,128)(2,1)S(1)}, bf16[2,136,128]{2,1,0:T(8,128)(2,1)S(1)}, u32[]{:S(2)}, u32[]{:S(2)}) collective-permute-start(bf16[2,136,128]{2,1,0:T(8,128)(2,1)S(1)} %get-tuple-element.85), channel_id=1, source_target_pairs={{0,16},{4,20},{8,24},{12,28},{16,0},{20,4},{24,8},{28,12},{1,17},{... | collective-permute-start | bytes 208904 | tf_op jit(solution)/shard_map/ppermute | solution.py:266
  19.8 6.5 %collective-permute-start.4 = (bf16[2,128,128]{2,1,0:T(8,128)(2,1)S(1)}, bf16[2,128,128]{2,1,0:T(8,128)(2,1)S(1)}, u32[]{:S(2)}, u32[]{:S(2)}) collective-permute-start(bf16[2,128,128]{2,1,0:T(8,128)(2,1)S(1)} %get-tuple-element.100), channel_id=1, source_target_pairs={{0,4},{4,0},{8,12},{12,8},{16,20},{20,16},{24,28},{28,24},{1,5},{5... | collective-permute-start | bytes 196616 | tf_op jit(solution)/shard_map/ppermute | solution.py:517
  19.8 6.4 %collective-permute-start.5 = (bf16[2,128,128]{2,1,0:T(8,128)(2,1)S(1)}, bf16[2,128,128]{2,1,0:T(8,128)(2,1)S(1)}, u32[]{:S(2)}, u32[]{:S(2)}) collective-permute-start(bf16[2,128,128]{2,1,0:T(8,128)(2,1)S(1)} %get-tuple-element.101), channel_id=1, source_target_pairs={{0,8},{4,12},{8,0},{12,4},{16,24},{20,28},{24,16},{28,20},{1,9},{5... | collective-permute-start | bytes 196616 | tf_op jit(solution)/shard_map/ppermute | solution.py:517
  21.1 5.2 %collective-permute-start.6 = (bf16[2,128,128]{2,1,0:T(8,128)(2,1)S(1)}, bf16[2,128,128]{2,1,0:T(8,128)(2,1)S(1)}, u32[]{:S(2)}, u32[]{:S(2)}) collective-permute-start(bf16[2,128,128]{2,1,0:T(8,128)(2,1)S(1)} %get-tuple-element.102), channel_id=1, source_target_pairs={{0,12},{4,8},{8,4},{12,0},{16,28},{20,24},{24,20},{28,16},{1,13},{... | collective-permute-start | bytes 196616 | tf_op jit(solution)/shard_map/ppermute | solution.py:517
  23.3 3.0 %copy-start = (f32[1024]{0:T(1024)S(1)}, f32[1024]{0:T(1024)}, u32[]{:S(2)}) copy-start(f32[1024]{0:T(1024)} %param.18) | copy-start | bytes 12292
  26.9 6.5 %collective-permute-start.9 = (bf16[256,1024]{1,0:T(8,128)(2,1)S(1)}, bf16[256,1024]{1,0:T(8,128)(2,1)S(1)}, u32[]{:S(2)}, u32[]{:S(2)}) collective-permute-start(bf16[256,1024]{1,0:T(8,128)(2,1)S(1)} %get-tuple-element.109), channel_id=1, source_target_pairs={{0,1},{1,0},{2,3},{3,2},{4,5},{5,4},{6,7},{7,6},{8,9},{9,8},{10,11... | collective-permute-start | bytes 1572872 | tf_op jit(solution)/shard_map/ppermute | solution.py:547
  42.7 9.6 %collective-permute-start.12 = (bf16[256,1024]{1,0:T(8,128)(2,1)S(1)}, bf16[256,1024]{1,0:T(8,128)(2,1)S(1)}, u32[]{:S(2)}, u32[]{:S(2)}) collective-permute-start(bf16[256,1024]{1,0:T(8,128)(2,1)S(1)} %get-tuple-element.126), channel_id=1, source_target_pairs={{0,1},{1,0},{2,3},{3,2},{4,5},{5,4},{6,7},{7,6},{8,9},{9,8},{10,11... | collective-permute-start | bytes 1572872 | tf_op jit(solution)/shard_map/ppermute | solution.py:547
  43.2 1.5 %collective-permute-start.7 = (f32[8,256]{1,0:T(8,128)S(1)}, f32[8,256]{1,0:T(8,128)S(1)}, u32[]{:S(2)}, u32[]{:S(2)}) collective-permute-start(f32[8,256]{1,0:T(8,128)S(1)} %get-tuple-element.107), channel_id=1, source_target_pairs={{0,1},{1,0},{2,3},{3,2},{4,5},{5,4},{6,7},{7,6},{8,9},{9,8},{10,11... | collective-permute-start | bytes 24584 | tf_op jit(solution)/shard_map/ppermute | solution.py:548
  44.8 14.9 %collective-permute-start.8 = (f32[8,256]{1,0:T(8,128)S(1)}, f32[8,256]{1,0:T(8,128)S(1)}, u32[]{:S(2)}, u32[]{:S(2)}) collective-permute-start(f32[8,256]{1,0:T(8,128)S(1)} %add.9), channel_id=1, source_target_pairs={{0,2},{1,3},{2,0},{3,1},{4,6},{5,7},{6,4},{7,5},{8,10},{9,11},{10,... | collective-permute-start | bytes 24584 | tf_op jit(solution)/shard_map/ppermute | solution.py:559
  46.3 29.9 %collective-permute-start.15 = (bf16[256,1280]{1,0:T(8,128)(2,1)S(1)}, bf16[256,1280]{1,0:T(8,128)(2,1)S(1)}, u32[]{:S(2)}, u32[]{:S(2)}) collective-permute-start(bf16[256,1280]{1,0:T(8,128)(2,1)S(1)} %product.7), channel_id=1, source_target_pairs={{0,2},{1,3},{2,0},{3,1},{4,6},{5,7},{6,4},{7,5},{8,10},{9,11},{10,... | collective-permute-start | bytes 1966088 | tf_op jit(solution)/shard_map/ppermute | solution.py:580
  46.8 19.9 %collective-permute-start.13 = (bf16[256,256]{1,0:T(8,128)(2,1)S(1)}, bf16[256,256]{1,0:T(8,128)(2,1)S(1)}, u32[]{:S(2)}, u32[]{:S(2)}) collective-permute-start(bf16[256,256]{1,0:T(8,128)(2,1)S(1)} %first.1), channel_id=1, source_target_pairs={{0,2},{1,3},{2,0},{3,1},{4,6},{5,7},{6,4},{7,5},{8,10},{9,11},{10,... | collective-permute-start | bytes 393224 | tf_op jit(solution)/shard_map/ppermute | solution.py:580
  48.3 26.8 %collective-permute-start.14 = (bf16[256,768]{1,0:T(8,128)(2,1)S(1)}, bf16[256,768]{1,0:T(8,128)(2,1)S(1)}, u32[]{:S(2)}, u32[]{:S(2)}) collective-permute-start(bf16[256,768]{1,0:T(8,128)(2,1)S(1)} %product.6), channel_id=1, source_target_pairs={{0,2},{1,3},{2,0},{3,1},{4,6},{5,7},{6,4},{7,5},{8,10},{9,11},{10,... | collective-permute-start | bytes 1179656 | tf_op jit(solution)/shard_map/ppermute | solution.py:580
  52.3 9.0 %collective-permute-start.11 = (f32[8,256]{1,0:T(8,128)S(1)}, f32[8,256]{1,0:T(8,128)S(1)}, u32[]{:S(2)}, u32[]{:S(2)}) collective-permute-start(f32[8,256]{1,0:T(8,128)S(1)} %get-tuple-element.123), channel_id=1, source_target_pairs={{0,1},{1,0},{2,3},{3,2},{4,5},{5,4},{6,7},{7,6},{8,9},{9,8},{10,11... | collective-permute-start | bytes 24584 | tf_op jit(solution)/shard_map/ppermute | solution.py:548
  59.7 23.8 %collective-permute-start.16 = (bf16[256,768]{1,0:T(8,128)(2,1)S(1)}, bf16[256,768]{1,0:T(8,128)(2,1)S(1)}, u32[]{:S(2)}, u32[]{:S(2)}) collective-permute-start(bf16[256,768]{1,0:T(8,128)(2,1)S(1)} %get-tuple-element.147), channel_id=1, source_target_pairs={{0,2},{1,3},{2,0},{3,1},{4,6},{5,7},{6,4},{7,5},{8,10},{9,11},{10,... | collective-permute-start | bytes 1179656 | tf_op jit(solution)/shard_map/ppermute | solution.py:580
  61.3 30.7 %collective-permute-start.17 = (bf16[256,768]{1,0:T(8,128)(2,1)S(1)}, bf16[256,768]{1,0:T(8,128)(2,1)S(1)}, u32[]{:S(2)}, u32[]{:S(2)}) collective-permute-start(bf16[256,768]{1,0:T(8,128)(2,1)S(1)} %get-tuple-element.150), channel_id=1, source_target_pairs={{0,2},{1,3},{2,0},{3,1},{4,6},{5,7},{6,4},{7,5},{8,10},{9,11},{10,... | collective-permute-start | bytes 1179656 | tf_op jit(solution)/shard_map/ppermute | solution.py:580
  66.7 27.2 %collective-permute-start.18 = (bf16[256,256]{1,0:T(8,128)(2,1)S(1)}, bf16[256,256]{1,0:T(8,128)(2,1)S(1)}, u32[]{:S(2)}, u32[]{:S(2)}) collective-permute-start(bf16[256,256]{1,0:T(8,128)(2,1)S(1)} %get-tuple-element.138), channel_id=1, source_target_pairs={{0,2},{1,3},{2,0},{3,1},{4,6},{5,7},{6,4},{7,5},{8,10},{9,11},{10,... | collective-permute-start | bytes 393224 | tf_op jit(solution)/shard_map/ppermute | solution.py:580
where the time goes:
time: 95.6 us; the launch traced here: 95 us
  Pallas kernels  46.6 us (49%)
  waiting for transfers between devices  29.5 us (31%)
  starting transfers between devices  18.3 us (19%)
    pallas_call x6, Pallas kernels, product(): pl.pallas_call(functools.partial(product_kernel, count=count), grid=(colu...  21.6 us
    ppermute x6, waiting for transfers between devices, local(): received[c].append(lax.ppermute(made[0], 'head', send))  19.5 us
    pallas_call x4, Pallas kernels, intra(): pl.pallas_call(functools.partial(intra_kernel, k=k, teams=teams, which=wh...  11.7 us
    ppermute x6, starting transfers between devices, around(): lax.ppermute(items[k], 'seq', [(i, i ^ k) for i in range(shards)])  7.69 us
    pallas_call x6, Pallas kernels, close(): pl.pallas_call(body, in_specs=in_specs, out_specs=ANYWHERE, out_shape=jax...  6.16 us
    ppermute x6, waiting for transfers between devices, around(): lax.ppermute(items[k], 'seq', [(i, i ^ k) for i in range(shards)])  5.21 us
    ppermute x6, starting transfers between devices, local(): received[c].append(lax.ppermute(made[0], 'head', send))  5.15 us
    pallas_call x1, Pallas kernels, states(): pl.pallas_call(functools.partial(state_kernel, width=width), in_specs=[AN...  3.59 us
  transfers between devices with their start and end apart: 19, of which 10 were waited for; matrix products, arithmetic and copies ran while one was open for 0% of the time, Pallas kernels for 35%

commit v1 on v0

--- a/solution.py
+++ b/solution.py
@@ -15,7 +15,7 @@
 BF16 = jnp.bfloat16
 PARAMS = pltpu.CompilerParams(vmem_limit_bytes=24 << 20)
 WHOLE = pltpu.CompilerParams(vmem_limit_bytes=60 * 1024 * 1024)
-CUTS = (1, 3, 5, 3, 3, 1)
+CUTS = (2, 4, 3, 3, 3, 1)
 ALONE = 3
 TAIL = 8
 RING = 4
@@ -67,72 +67,96 @@
     return copies
 
 
-def state_kernel(rate_any, skip_any, dt_any, resets_any, b_any, c_any, x_any, *refs, width):
-    place_ref = where_am_i()
-    pay_refs, tables, scratch = refs[:RING], refs[RING : RING + 8], refs[RING + 8 :]
-    start_ref, reach_ref, b_ref, c_ref, row_ref, count_ref, flip_ref, skip_ref = tables
-    rate_s, skip_s, dt_s, resets_s, x_s, w_s, bt_s, thr_s, sems = scratch
+def fetch(sems, pairs):
+    copies = [pltpu.make_async_copy(src, dst, sems.at[i]) for i, (src, dst) in enumerate(pairs)]
+    for copy in copies:
+        copy.start()
+    return copies
+
+
+def quarter_states(quarter, x_ref, pay_ref, start_ref, reach_ref, w_ref, bt_ref, thr_ref, width):
     blocks, state, channels = start_ref.shape
     wide = channels // RING
     pairs = wide // LANES
-    quarters = [place_ref[1] ^ k for k in range(RING)]
-    moves = [(dt_any, dt_s), (resets_any, resets_s), (rate_any, rate_s), (skip_any, skip_s), (b_any, b_ref)]
-    moves += [(x_any.at[:, pl.ds(pl.multiple_of(q * wide, wide), wide)], x_s.at[k]) for k, q in enumerate(quarters)]
-    moves.append((c_any, c_ref))
+    two = 4 * pairs
+    own = pl.ds(pl.multiple_of(quarter // 2 * two, two), two)
+    odd = quarter % 2 == 1
+
+    def rows_of(ref, cols):
+        both = ref[own, cols]
+        return jnp.where(odd, both[two // 2 :], both[: two // 2])
+
+    for i in range(pairs):
+        lanes = pl.ds(pl.multiple_of(quarter * wide + i * LANES, LANES), LANES)
+        running = jnp.zeros((state, LANES), F32)
+        product = jnp.ones((1, LANES), F32)
+        for b in range(blocks):
+            cols = slice(b * SPAN, (b + 1) * SPAN)
+            start_ref[b, :, lanes] = running.astype(BF16)
+            reach_ref[b, :, lanes] = jnp.broadcast_to(product, (8, LANES))
+            x = x_ref[cols, i * LANES : (i + 1) * LANES]
+            rows = rows_of(w_ref, cols)
+            parts = []
+            for j in range(2):
+                left = (bt_ref[:, cols] * rows[2 * i + j : 2 * i + j + 1]).astype(BF16)
+                parts.append(jnp.dot(left, x, preferred_element_type=F32))
+            fresh = halves(parts[0], parts[1], (state, LANES), width)
+            thr = rows_of(thr_ref, slice(b * LANES, (b + 1) * LANES))
+            thr = halves(thr[2 * i : 2 * i + 1], thr[2 * i + 1 : 2 * i + 2], (1, LANES), width)
+            running = thr * running + fresh
+            product = product * thr
+        pay_ref[i, :state, :] = running.astype(BF16)
+        pay_ref[i, state:, :] = split(product)
+
+
+def state_kernel(rate_any, dt_any, resets_any, b_any, c_any, x_any, *refs, width):
+    pay_refs, shared, scratch = refs[: RING - 1], refs[RING - 1 : RING + 10], refs[RING + 10 :]
+    start_ref, reach_ref, b_ref, c_ref, count_ref, cum_ref, scale_ref, x_ref, w_ref, bt_ref, thr_ref = shared
+    rate_s, dt_s, resets_s, x_s, sems = scratch
+    blocks, _, channels = start_ref.shape
+    wide = channels // RING
+    quarters = [where_am_i()[1] ^ k for k in range(RING)]
+    at = lambda q: pl.ds(pl.multiple_of(q * wide, wide), wide)
+    moves = [(dt_any, dt_s), (resets_any, resets_s), (rate_any, rate_s), (b_any, b_ref)]
+    moves += [(x_any.at[:, at(q)], x_s.at[k]) for k, q in enumerate(quarters[1:])]
+    moves += [(x_any.at[:, at(quarters[0])], x_ref), (c_any, c_ref)]
     copies = fetch(sems, moves)
-    for copy in copies[:4]:
+    for copy in copies[:3]:
         copy.wait()
     scale, cum, count = prep(dt_s[...], rate_s[...], resets_s[...])
+    scale_ref[...], cum_ref[...], count_ref[...] = scale, cum, count
     heads = cum.shape[0]
     for b in range(blocks):
         cols = slice(b * SPAN, (b + 1) * SPAN)
         c, n = cum[:, cols], count[:1, cols]
         end, last = c[:, SPAN - 1 :], n[:, SPAN - 1 :]
-        w_s[:, cols] = jnp.where(n == last, jnp.exp2(end - c), 0.0) * scale[:, cols]
+        w_ref[:, cols] = jnp.where(n == last, jnp.exp2(end - c), 0.0) * scale[:, cols]
         through = jnp.where(last == 0.0, jnp.exp2(end), 0.0)
-        thr_s[:, b * LANES : (b + 1) * LANES] = jnp.broadcast_to(through, (heads, LANES))
-    copies[4].wait()
-    bt_s[...] = b_ref[...].astype(F32).T
-    two = 4 * pairs
-    for k, quarter in enumerate(quarters):
-        own = pl.ds(pl.multiple_of(quarter // 2 * two, two), two)
-        odd = quarter % 2 == 1
-
-        def rows_of(ref, cols):
-            both = ref[own, cols]
-            return jnp.where(odd, both[two // 2 :], both[: two // 2])
-
-        copies[5 + k].wait()
-        for i in range(pairs):
-            lanes = pl.ds(pl.multiple_of(quarter * wide + i * LANES, LANES), LANES)
-            running = jnp.zeros((state, LANES), F32)
-            product = jnp.ones((1, LANES), F32)
-            for b in range(blocks):
-                cols = slice(b * SPAN, (b + 1) * SPAN)
-                start_ref[b, :, lanes] = running.astype(BF16)
-                reach_ref[b, :, lanes] = jnp.broadcast_to(product, (8, LANES))
-                x = x_s[k, cols, i * LANES : (i + 1) * LANES]
-                rows = rows_of(w_s, cols)
-                parts = []
-                for j in range(2):
-                    left = (bt_s[:, cols] * rows[2 * i + j : 2 * i + j + 1]).astype(BF16)
-                    parts.append(jnp.dot(left, x, preferred_element_type=F32))
-                fresh = halves(parts[0], parts[1], (state, LANES), width)
-                thr = rows_of(thr_s, slice(b * LANES, (b + 1) * LANES))
-                thr = halves(thr[2 * i : 2 * i + 1], thr[2 * i + 1 : 2 * i + 2], (1, LANES), width)
-                running = thr * running + fresh
-                product = product * thr
-            pay_refs[k][i, :state, :] = running.astype(BF16)
-            pay_refs[k][i, state:, :] = split(product)
-    row_ref[...] = cum - jnp.log2(scale)
-    count_ref[...] = count
-    skip_ref[...] = jnp.broadcast_to(column_of(skip_s[...]), (heads, LANES))
+        thr_ref[:, b * LANES : (b + 1) * LANES] = jnp.broadcast_to(through, (heads, LANES))
+    copies[3].wait()
+    bt_ref[...] = b_ref[...].astype(F32).T
+    for k, quarter in enumerate(quarters[1:]):
+        copies[4 + k].wait()
+        quarter_states(quarter, x_s.at[k], pay_refs[k], start_ref, reach_ref, w_ref, bt_ref, thr_ref, width)
+    for copy in copies[RING + 3 :]:
+        copy.wait()
+
+
+def table_kernel(skip_any, start_in, reach_in, count_ref, cum_ref, scale_ref, x_ref, w_ref, bt_ref, thr_ref, *refs, width):
+    pay_ref, start_ref, reach_ref, row_ref, flip_ref, skip_ref, skip_s, sems = refs
+    blocks = start_ref.shape[0]
+    copies = fetch(sems, [(skip_any, skip_s)])
+    quarter_states(where_am_i()[1], x_ref, pay_ref, start_ref, reach_ref, w_ref, bt_ref, thr_ref, width)
+    cum, count = cum_ref[...], count_ref[...]
+    heads = cum.shape[0]
+    row_ref[...] = cum - jnp.log2(scale_ref[...])
     start = jnp.where(count[:1] == 0.0, jnp.exp2(cum), 0.0)
     for b in range(blocks):
         cols = slice(b * SPAN, (b + 1) * SPAN)
         stack = [cum[:, cols], start[:, cols], count[:, cols], jnp.zeros((LANES - 2 * heads - 8, SPAN), F32)]
         flip_ref[b] = jnp.concatenate(stack, axis=0).T
-    copies[5 + RING].wait()
+    copies[0].wait()
+    skip_ref[...] = jnp.broadcast_to(column_of(skip_s[...]), (heads, LANES))
 
 
 def split(product):
@@ -153,41 +177,65 @@
 ANYWHERE = pl.BlockSpec(memory_space=pl.ANY)
 
 
-def states(dt, rate, skip, resets, bmat, cmat, xs, blocks, width):
+def states(dt, rate, resets, bmat, cmat, xs, blocks, width):
     tokens, channels = xs.shape
     heads, state = dt.shape[0], bmat.shape[1]
     wide = channels // RING
     pay = (wide // LANES, state + TAIL, LANES)
     return pl.pallas_call(
         functools.partial(state_kernel, width=width),
-        in_specs=[ANYWHERE] * 7,
-        out_specs=[VECTORS] * (RING + 8),
+        in_specs=[ANYWHERE] * 6,
+        out_specs=[VECTORS] * (RING + 10),
         scratch_shapes=[
-            pltpu.VMEM((1, heads), F32),
             pltpu.VMEM((1, heads), F32),
             pltpu.VMEM((heads, tokens), jnp.int32),
             pltpu.VMEM((1, tokens), jnp.int32),
-            pltpu.VMEM((RING, tokens, wide), BF16),
-            pltpu.VMEM((heads, tokens), F32),
-            pltpu.VMEM((state, tokens), F32),
-            pltpu.VMEM((heads, blocks * LANES), F32),
-            pltpu.SemaphoreType.DMA((6 + RING,)),
+            pltpu.VMEM((RING - 1, tokens, wide), BF16),
+            pltpu.SemaphoreType.DMA((RING + 5,)),
         ],
         out_shape=[
-            *[jax.ShapeDtypeStruct(pay, BF16)] * RING,
+            *[jax.ShapeDtypeStruct(pay, BF16)] * (RING - 1),
             jax.ShapeDtypeStruct((blocks, state, channels), BF16),
             jax.ShapeDtypeStruct((blocks, 8, channels), F32),
             jax.ShapeDtypeStruct((tokens, state), BF16),
             jax.ShapeDtypeStruct((tokens, state), BF16),
+            jax.ShapeDtypeStruct((8, tokens), F32),
             jax.ShapeDtypeStruct((heads, tokens), F32),
-            jax.ShapeDtypeStruct((8, tokens), F32),
+            jax.ShapeDtypeStruct((heads, tokens), F32),
+            jax.ShapeDtypeStruct((tokens, wide), BF16),
+            jax.ShapeDtypeStruct((heads, tokens), F32),
+            jax.ShapeDtypeStruct((state, tokens), F32),
+            jax.ShapeDtypeStruct((heads, blocks * LANES), F32),
+        ],
+        cost_estimate=pl.CostEstimate(flops=3 * tokens * channels * state, bytes_accessed=4 << 20, transcendentals=tokens * heads),
+        compiler_params=PARAMS,
+        name="states",
+    )(rate, dt, resets, bmat, cmat, xs)
+
+
+def tables_of(skip, starts, reach, count, cum, scale, x, w, bt, thr, width):
+    heads, tokens = cum.shape
+    blocks, state, _ = starts.shape
+    pay = (x.shape[1] // LANES, state + TAIL, LANES)
+    shape = lambda a: jax.ShapeDtypeStruct(a.shape, a.dtype)
+    return pl.pallas_call(
+        functools.partial(table_kernel, width=width),
+        in_specs=[ANYWHERE] + [VECTORS] * 9,
+        out_specs=[VECTORS] * 6,
+        scratch_shapes=[pltpu.VMEM((1, heads), F32), pltpu.SemaphoreType.DMA((1,))],
+        out_shape=[
+            jax.ShapeDtypeStruct(pay, BF16),
+            shape(starts),
+            shape(reach),
+            shape(cum),
             jax.ShapeDtypeStruct((blocks, SPAN, LANES), F32),
             jax.ShapeDtypeStruct((heads, LANES), F32),
         ],
-        cost_estimate=pl.CostEstimate(flops=4 * tokens * channels * state, bytes_accessed=4 << 20, transcendentals=tokens * heads),
-        compiler_params=PARAMS,
-        name="states",
-    )(rate, skip, dt, resets, bmat, cmat, xs)
+        input_output_aliases={1: 1, 2: 2},
+        cost_estimate=pl.CostEstimate(flops=tokens * x.shape[1] * state * 4, bytes_accessed=4 << 20, transcendentals=tokens * heads),
+        compiler_params=PARAMS,
+        name="tables",
+    )(skip, starts, reach, count, cum, scale, x, w, bt, thr)
 
 
 def swapped(items, mine):
@@ -508,7 +556,7 @@
         return lax.optimization_barrier((value, *others))[0]
 
     def inside(k, which, when):
-        columns = CUTS[0] * unit if (k, which) == (0, 1) else 0
+        columns = CUTS[0] * unit if (k, which) == (1, 0) else 0
         return intra(k, teams, which, (when, *tables), xs, gate, weight, columns, width)
 
     def around(items):
@@ -517,24 +565,27 @@
             got.append(lax.ppermute(items[k], "seq", [(i, i ^ k) for i in range(shards)]))
         return got
 
-    *pays, starts, reach, keys, queries, row, count, flip, direct = states(
-        dt, decay_rate, skip, flags, bmat, cmat, xs, blocks, width
+    *pays, starts, reach, keys, queries, count, cum, scale, x, w, bt, thr = states(
+        dt, decay_rate, flags, bmat, cmat, xs, blocks, width
+    )
+    first, starts, reach, row, flip, direct = tables_of(
+        after(skip, pays[0]), starts, reach, count, cum, scale, x, w, bt, thr, width
     )
     tables = (keys, queries, row, count, flip)
     weight_b = lax.ppermute(after(raw, pays[0]), "head", swap)
-    gathered = around(pays)
+    gathered = around([first, *pays])
     locals_ = {}
-    early = after(direct, pays[0])
-    for k in range(1, teams):
-        locals_[k, 1] = inside(k, 1, early)
     total, before, ahead = prefix(gathered)
     left = across(total, rings)
     early = after(direct, total)
     for k in range(1, teams):
-        locals_[k, 0] = inside(k, 0, early)
+        locals_[k, 1] = inside(k, 1, early)
     outgoing = spread(left, before, ahead, rings > 2)
     incoming = around(outgoing)
-    *locals_[0, 1], ready = inside(0, 1, after(direct, outgoing[0]))
+    early = after(direct, outgoing[0])
+    for k in range(1, teams):
+        locals_[k, 0] = inside(k, 0, early)
+    *locals_[1, 0], ready = locals_[1, 0]
 
     def pair_of(k, when):
         done = []

time: 95.6 us -> 94.8 us (level)
  waiting for transfers between devices: 29.5 us -> 28.1 us
    ppermute x6, waiting for transfers between devices: 5.21 us -> 4.15 us  [around(): lax.ppermute(items[k], 'seq', [(i, i ^ k) for i in range(shards)])]
    pallas_call x0 -> x1, Pallas kernels: none -> 1.03 us  [tables_of(): pl.pallas_call(functools.partial(table_kernel, width=width), in_specs=[AN...]
    pallas_call x6, Pallas kernels: 21.6 us -> 20.6 us  [product(): pl.pallas_call(functools.partial(product_kernel, count=count), grid=(colu...]
  transfers between devices with their start and end apart: 19 -> 19, of which waited for: 10 -> 10; matrix products, arithmetic and copies ran while one was open for 0% -> 0% of each run, Pallas kernels for 35% -> 33%
where the time goes in v1:
time: 94.8 us; the launch traced here: 94.2 us
  Pallas kernels  46.4 us (49%)
  waiting for transfers between devices  28.1 us (30%)
  starting transfers between devices  19.1 us (20%)
    pallas_call x6, Pallas kernels, product(): pl.pallas_call(functools.partial(product_kernel, count=count), grid=(colu...  20.6 us
    ppermute x6, waiting for transfers between devices, local(): received[c].append(lax.ppermute(made[0], 'head', send))  18.7 us
    pallas_call x4, Pallas kernels, intra(): pl.pallas_call(functools.partial(intra_kernel, k=k, teams=teams, which=wh...  11.7 us
    ppermute x6, starting transfers between devices, around(): lax.ppermute(items[k], 'seq', [(i, i ^ k) for i in range(shards)])  7.73 us
    pallas_call x6, Pallas kernels, close(): pl.pallas_call(body, in_specs=in_specs, out_specs=ANYWHERE, out_shape=jax...  6.15 us
    ppermute x6, starting transfers between devices, local(): received[c].append(lax.ppermute(made[0], 'head', send))  5.89 us
    ppermute x6, waiting for transfers between devices, around(): lax.ppermute(items[k], 'seq', [(i, i ^ k) for i in range(shards)])  4.15 us
    ppermute x1, waiting for transfers between devices, across(): lax.ppermute(send, 'seq', [(i, i ^ RING * level) for i in range(shards)])  3.78 us
  transfers between devices with their start and end apart: 19, of which 10 were waited for; matrix products, arithmetic and copies ran while one was open for 0% of the time, Pallas kernels for 33%

profile of v1, /device:TPU:0, one launch (start us, length us, event | category | flops | bytes accessed | tf_op | source)
XLA Modules:
  0.0 94.2 jit_solution(16837014340364248938)
XLA Ops:
  0.0 3.1 %states.1 = (bf16[2,136,128]{2,1,0:T(8,128)(2,1)S(1)}, bf16[2,136,128]{2,1,0:T(8,128)(2,1)S(1)}, bf16[2,136,128]{2,1,0:T(8,128)(2,1)S(1)}, bf16[4,128,1024]{2,1,...) custom-call(f32[1,16]{1,0:T(1,128)} %bitcast.9, ...), custom_call_target="tpu_custom_call" | custom-call | flops 402653184 | bytes 4194304 | tf_op jit(solution)/shard_map/states/pallas_call | solution.py:185
  3.2 0.6 collective-permute-start.10
  3.7 2.6 %collective-permute-start.1 = (bf16[2,136,128]{2,1,0:T(8,128)(2,1)S(1)}, bf16[2,136,128]{2,1,0:T(8,128)(2,1)S(1)}, u32[]{:S(2)}, u32[]{:S(2)}) collective-permute-start(bf16[2,136,128]{2,1,0:T(8,128)(2,1)S(1)} %get-tuple-element.101), channel_id=1, source_target_pairs={{0,8},{4,12},{8,0},{12,4},{16,24},{20,28},{24,16},{28,20},{1,9},{5... | collective-permute-start | bytes 208904 | tf_op jit(solution)/shard_map/ppermute | solution.py:565
  6.3 1.4 %collective-permute-start.2 = (bf16[2,136,128]{2,1,0:T(8,128)(2,1)S(1)}, bf16[2,136,128]{2,1,0:T(8,128)(2,1)S(1)}, u32[]{:S(2)}, u32[]{:S(2)}) collective-permute-start(bf16[2,136,128]{2,1,0:T(8,128)(2,1)S(1)} %get-tuple-element.102), channel_id=1, source_target_pairs={{0,12},{4,8},{8,4},{12,0},{16,28},{20,24},{24,20},{28,16},{1,13},{... | collective-permute-start | bytes 208904 | tf_op jit(solution)/shard_map/ppermute | solution.py:565
  7.9 1.0 %tables.1 = (bf16[2,136,128]{2,1,0:T(8,128)(2,1)S(1)}, bf16[4,128,1024]{2,1,0:T(8,128)(2,1)S(1)}, f32[4,8,1024]{2,1,0:T(8,128)S(1)}, f32[16,1024]{1,0:T(8,128)S(...) custom-call(f32[1,16]{1,0:T(1,128)} %bitcast.10, ...), custom_call_target="tpu_custom_call", output_to_operand_aliasing={{1}: (1, {}), {2}: (2, {})} | custom-call | flops 134217728 | bytes 4194304 | tf_op jit(solution)/shard_map/tables/pallas_call | solution.py:221
  9.1 2.7 %collective-permute-done.2.refs_3_ = bf16[2,136,128]{2,1,0:T(8,128)(2,1)S(1)} collective-permute-done((bf16[2,136,128]{2,1,0:T(8,128)(2,1)S(1)}, bf16[2,136,128]{2,1,0:T(8,128)(2,1)S(1)}, u32[]{:S(2)}, u32[]{:S(2)}) %collective-permute-start.2) | collective-permute-done | bytes 69664 | tf_op jit(solution)/shard_map/ppermute | solution.py:565
  11.8 1.3 %collective-permute-done.refs_1_ = bf16[2,136,128]{2,1,0:T(8,128)(2,1)S(1)} collective-permute-done((bf16[2,136,128]{2,1,0:T(8,128)(2,1)S(1)}, bf16[2,136,128]{2,1,0:T(8,128)(2,1)S(1)}, u32[]{:S(2)}, u32[]{:S(2)}) %collective-permute-start) | collective-permute-done | bytes 69664 | tf_op jit(solution)/shard_map/ppermute | solution.py:565
  13.1 0.2 prefix.1
  13.3 2.6 %collective-permute-start.3 = (bf16[2,136,128]{2,1,0:T(8,128)(2,1)S(1)}, bf16[2,136,128]{2,1,0:T(8,128)(2,1)S(1)}, u32[]{:S(2)}, u32[]{:S(2)}) collective-permute-start(bf16[2,136,128]{2,1,0:T(8,128)(2,1)S(1)} %get-tuple-element.103), channel_id=1, source_target_pairs={{0,16},{4,20},{8,24},{12,28},{16,0},{20,4},{24,8},{28,12},{1,17},{... | collective-permute-start | bytes 208904 | tf_op jit(solution)/shard_map/ppermute | solution.py:314
  15.9 3.8 %collective-permute-done.3.left_ref = bf16[2,136,128]{2,1,0:T(8,128)(2,1)S(1)} collective-permute-done((bf16[2,136,128]{2,1,0:T(8,128)(2,1)S(1)}, bf16[2,136,128]{2,1,0:T(8,128)(2,1)S(1)}, u32[]{:S(2)}, u32[]{:S(2)}) %collective-permute-start.3) | collective-permute-done | bytes 69664 | tf_op jit(solution)/shard_map/ppermute | solution.py:314
  19.8 0.7 collective-permute-start.4
  20.5 0.2 collective-permute-start.5
  20.7 2.6 %collective-permute-start.6 = (bf16[2,128,128]{2,1,0:T(8,128)(2,1)S(1)}, bf16[2,128,128]{2,1,0:T(8,128)(2,1)S(1)}, u32[]{:S(2)}, u32[]{:S(2)}) collective-permute-start(bf16[2,128,128]{2,1,0:T(8,128)(2,1)S(1)} %get-tuple-element.119), channel_id=1, source_target_pairs={{0,12},{4,8},{8,4},{12,0},{16,28},{20,24},{24,20},{28,16},{1,13},{... | collective-permute-start | bytes 196616 | tf_op jit(solution)/shard_map/ppermute | solution.py:565
  23.3 2.9 %intra.5 = (f32[256,1024]{1,0:T(8,128)S(1)}, bf16[256,1024]{1,0:T(8,128)(2,1)S(1)}) custom-call(f32[16,128]{1,0:T(8,128)S(1)} %get-tuple-element.132.skip_ref, bf16[1024,128]{1,0:T(8,128)(2,1)S(1)} %get-tuple-element.108.b_ref, bf16[1024,128]{1,0:T(8,128)(2,1)S(1)} %get-tuple-element.109.c_ref, f32[16,1024]{1,0:T(8,128)S(1)} %get-tuple-element.110.row_ref, ...), custom_call_target="tpu_custom_call" | custom-call | flops 536870912 | bytes 2097152 | tf_op jit(solution)/shard_map/intra/pallas_call | solution.py:385
  26.3 0.6 finish.5
  26.9 3.0 %intra.4 = (f32[256,1024]{1,0:T(8,128)S(1)}, bf16[256,1024]{1,0:T(8,128)(2,1)S(1)}, bf16[1024,512]{1,0:T(8,128)(2,1)S(1)}) custom-call(f32[16,128]{1,0:T(8,128)S(1)} %get-tuple-element.132.skip_ref, bf16[1024,128]{1,0:T(8,128)(2,1)S(1)} %get-tuple-element.108.b_ref, bf16[1024,128]{1,0:T(8,128)(2,1)S(1)} %get-tuple-element.109.c_ref, ...), custom_call_target="tpu_custom_call" | custom-call | flops 536870912 | bytes 2097152 | tf_op jit(solution)/shard_map/intra/pallas_call | solution.py:385
  29.9 0.6 finish.4
  30.5 1.2 %first.1 = bf16[256,512]{1,0:T(8,128)(2,1)S(1)} custom-call(bf16[256,1024]{1,0:T(8,128)(2,1)S(1)} %get-tuple-element.148.a_ref.refs_0_, bf16[256,1024]{1,0:T(8,128)(2,1)S(1)} %collective-permute-done.9.b_ref.refs_1_, bf16[1024,512]{1,0:T(8,128)(2,1)S(1)} %get-tuple-element.127.wa_ref, bf16[1024,4096]{1,0:T(8,128)(2,1)S(1)} %collective-permute-done.10.wb_any.refs_3_.refs_5_), custom_call_target="tpu_custom_call" | custom-call | flops 536870912 | bytes 2097152 | tf_op jit(solution)/shard_map/first/pallas_call | solution.py:484
  31.7 3.6 %product.6 = bf16[256,1024]{1,0:T(8,128)(2,1)S(1)} custom-call(bf16[256,1024]{1,0:T(8,128)(2,1)S(1)} %get-tuple-element.148.a_ref.refs_0_, bf16[256,1024]{1,0:T(8,128)(2,1)S(1)} %collective-permute-done.9.b_ref.refs_1_, bf16[1024,4096]{1,0:T(8,128)(2,1)} %refs_2_.5, bf16[1024,4096]{1,0:T(8,128)(2,1)S(1)} %collective-permute-done.10.wb_any.refs_3_.refs_5_), custom_call_target="tpu_custom_call" | custom-call | flops 1073741824 | bytes 4194304 | tf_op jit(solution)/shard_map/product/pallas_call | solution.py:456
  35.4 3.0 %product.7 = bf16[256,768]{1,0:T(8,128)(2,1)S(1)} custom-call(bf16[256,1024]{1,0:T(8,128)(2,1)S(1)} %get-tuple-element.148.a_ref.refs_0_, bf16[256,1024]{1,0:T(8,128)(2,1)S(1)} %collective-permute-done.9.b_ref.refs_1_, bf16[1024,4096]{1,0:T(8,128)(2,1)} %refs_2_.5, bf16[1024,4096]{1,0:T(8,128)(2,1)S(1)} %collective-permute-done.10.wb_any.refs_3_.refs_5_), custom_call_target="tpu_custom_call" | custom-call | flops 805306368 | bytes 3145728 | tf_op jit(solution)/shard_map/product/pallas_call | solution.py:456
  38.4 2.9 %intra.7 = (f32[256,1024]{1,0:T(8,128)S(1)}, bf16[256,1024]{1,0:T(8,128)(2,1)S(1)}) custom-call(f32[16,128]{1,0:T(8,128)S(1)} %get-tuple-element.132.skip_ref, bf16[1024,128]{1,0:T(8,128)(2,1)S(1)} %get-tuple-element.108.b_ref, bf16[1024,128]{1,0:T(8,128)(2,1)S(1)} %get-tuple-element.109.c_ref, f32[16,1024]{1,0:T(8,128)S(1)} %get-tuple-element.110.row_ref, ...), custom_call_target="tpu_custom_call" | custom-call | flops 536870912 | bytes 2097152 | tf_op jit(solution)/shard_map/intra/pallas_call | solution.py:385
  41.4 0.6 finish.7
  41.9 0.5 collective-permute-start.12
  42.5 1.5 %collective-permute-done.7 = f32[8,256]{1,0:T(8,128)S(1)} collective-permute-done((f32[8,256]{1,0:T(8,128)S(1)}, f32[8,256]{1,0:T(8,128)S(1)}, u32[]{:S(2)}, u32[]{:S(2)}) %collective-permute-start.7) | collective-permute-done | bytes 8224 | tf_op jit(solution)/shard_map/ppermute | solution.py:599
  44.0 1.5 %collective-permute-start.8 = (f32[8,256]{1,0:T(8,128)S(1)}, f32[8,256]{1,0:T(8,128)S(1)}, u32[]{:S(2)}, u32[]{:S(2)}) collective-permute-start(f32[8,256]{1,0:T(8,128)S(1)} %add.9), channel_id=1, source_target_pairs={{0,2},{1,3},{2,0},{3,1},{4,6},{5,7},{6,4},{7,5},{8,10},{9,11},{10,... | collective-permute-start | bytes 24584 | tf_op jit(solution)/shard_map/ppermute | solution.py:610
  45.5 0.5 collective-permute-start.15
  46.0 1.5 %collective-permute-start.13 = (bf16[256,512]{1,0:T(8,128)(2,1)S(1)}, bf16[256,512]{1,0:T(8,128)(2,1)S(1)}, u32[]{:S(2)}, u32[]{:S(2)}) collective-permute-start(bf16[256,512]{1,0:T(8,128)(2,1)S(1)} %first.1), channel_id=1, source_target_pairs={{0,2},{1,3},{2,0},{3,1},{4,6},{5,7},{6,4},{7,5},{8,10},{9,11},{10,... | collective-permute-start | bytes 786440 | tf_op jit(solution)/shard_map/ppermute | solution.py:631
  47.5 0.5 collective-permute-start.14
  48.1 2.9 %intra.6 = (f32[256,1024]{1,0:T(8,128)S(1)}, bf16[256,1024]{1,0:T(8,128)(2,1)S(1)}) custom-call(f32[16,128]{1,0:T(8,128)S(1)} %get-tuple-element.132.skip_ref, bf16[1024,128]{1,0:T(8,128)(2,1)S(1)} %get-tuple-element.108.b_ref, bf16[1024,128]{1,0:T(8,128)(2,1)S(1)} %get-tuple-element.109.c_ref, f32[16,1024]{1,0:T(8,128)S(1)} %get-tuple-element.110.row_ref, ...), custom_call_target="tpu_custom_call" | custom-call | flops 536870912 | bytes 2097152 | tf_op jit(solution)/shard_map/intra/pallas_call | solution.py:385
  51.0 0.6 finish.6
  51.6 3.6 %product.8 = (bf16[256,768]{1,0:T(8,128)(2,1)S(1)}, f32[256,768]{1,0:T(8,128)S(1)}) custom-call(bf16[256,1024]{1,0:T(8,128)(2,1)S(1)} %get-tuple-element.148.a_ref.refs_0_, bf16[256,1024]{1,0:T(8,128)(2,1)S(1)} %collective-permute-done.9.b_ref.refs_1_, bf16[256,1024]{1,0:T(8,128)(2,1)S(1)} %get-tuple-element.155.refs_2_.refs_0_, ...), custom_call_target="tpu_custom_call" | custom-call | flops 1610612736 | bytes 3145728 | tf_op jit(solution)/shard_map/product/pallas_call | solution.py:456
  55.3 3.6 %product.9 = (bf16[256,768]{1,0:T(8,128)(2,1)S(1)}, f32[256,768]{1,0:T(8,128)S(1)}) custom-call(bf16[256,1024]{1,0:T(8,128)(2,1)S(1)} %get-tuple-element.148.a_ref.refs_0_, bf16[256,1024]{1,0:T(8,128)(2,1)S(1)} %collective-permute-done.9.b_ref.refs_1_, bf16[256,1024]{1,0:T(8,128)(2,1)S(1)} %get-tuple-element.155.refs_2_.refs_0_, ...), custom_call_target="tpu_custom_call" | custom-call | flops 1610612736 | bytes 3145728 | tf_op jit(solution)/shard_map/product/pallas_call | solution.py:456
  58.9 1.6 %collective-permute-start.16 = (bf16[256,768]{1,0:T(8,128)(2,1)S(1)}, bf16[256,768]{1,0:T(8,128)(2,1)S(1)}, u32[]{:S(2)}, u32[]{:S(2)}) collective-permute-start(bf16[256,768]{1,0:T(8,128)(2,1)S(1)} %get-tuple-element.163), channel_id=1, source_target_pairs={{0,2},{1,3},{2,0},{3,1},{4,6},{5,7},{6,4},{7,5},{8,10},{9,11},{10,... | collective-permute-start | bytes 1179656 | tf_op jit(solution)/shard_map/ppermute | solution.py:631
  60.5 0.5 collective-permute-start.17
  61.0 1.8 %product.10 = (bf16[256,256]{1,0:T(8,128)(2,1)S(1)}, f32[256,256]{1,0:T(8,128)S(1)}) custom-call(bf16[256,1024]{1,0:T(8,128)(2,1)S(1)} %get-tuple-element.148.a_ref.refs_0_, bf16[256,1024]{1,0:T(8,128)(2,1)S(1)} %collective-permute-done.9.b_ref.refs_1_, bf16[256,1024]{1,0:T(8,128)(2,1)S(1)} %get-tuple-element.155.refs_2_.refs_0_, ...), custom_call_target="tpu_custom_call" | custom-call | flops 536870912 | bytes 1048576 | tf_op jit(solution)/shard_map/product/pallas_call | solution.py:456
  62.8 0.3 collective-permute-done.13.refs_2_
  63.1 1.3 %collective-permute-start.18 = (bf16[256,256]{1,0:T(8,128)(2,1)S(1)}, bf16[256,256]{1,0:T(8,128)(2,1)S(1)}, u32[]{:S(2)}, u32[]{:S(2)}) collective-permute-start(bf16[256,256]{1,0:T(8,128)(2,1)S(1)} %get-tuple-element.154), channel_id=1, source_target_pairs={{0,2},{1,3},{2,0},{3,1},{4,6},{5,7},{6,4},{7,5},{8,10},{9,11},{10,... | collective-permute-start | bytes 393224 | tf_op jit(solution)/shard_map/ppermute | solution.py:631
  64.4 4.9 %product.11 = f32[256,2304]{1,0:T(8,128)S(1)} custom-call(bf16[256,1024]{1,0:T(8,128)(2,1)S(1)} %get-tuple-element.155.refs_2_.refs_0_, bf16[256,1024]{1,0:T(8,128)(2,1)S(1)} %collective-permute-done.12.refs_3_.refs_1_, bf16[1024,4096]{1,0:T(8,128)(2,1)} %refs_2_.5, bf16[1024,4096]{1,0:T(8,128)(2,1)S(1)} %collective-permute-done.10.wb_any.refs_3_.refs_5_), custom_call_target="tpu_custom_call" | custom-call | flops 2415919104 | bytes 9437184 | tf_op jit(solution)/shard_map/product/pallas_call | solution.py:456
  69.5 1.0 %close.6.refs_3_ = bf16[256,4096]{1,0:T(8,128)(2,1)} custom-call(f32[8,256]{1,0:T(8,128)S(1)} %add_add_fusion.refs_0_, f32[256,512]{1,0:T(8,128)S(1)} %slice.14.refs_1_, bf16[256,512]{1,0:T(8,128)(2,1)S(1)} %collective-permute-done.13.refs_2_), custom_call_target="tpu_custom_call" | custom-call | flops 524288 | bytes 1048576 | tf_op jit(solution)/shard_map/close/pallas_call | solution.py:524
  70.5 3.8 %collective-permute-done.14.refs_2_ = bf16[256,1024]{1,0:T(8,128)(2,1)S(1)} collective-permute-done((bf16[256,1024]{1,0:T(8,128)(2,1)S(1)}, bf16[256,1024]{1,0:T(8,128)(2,1)S(1)}, u32[]{:S(2)}, u32[]{:S(2)}) %collective-permute-start.14) | collective-permute-done | bytes 524320 | tf_op jit(solution)/shard_map/ppermute | solution.py:631
  74.4 1.1 %close.7.refs_3_ = bf16[256,4096]{1,0:T(8,128)(2,1)} custom-call(f32[8,256]{1,0:T(8,128)S(1)} %add_add_fusion.refs_0_, f32[256,1024]{1,0:T(8,128)S(1)} %slice.13.refs_1_, bf16[256,1024]{1,0:T(8,128)(2,1)S(1)} %collective-permute-done.14.refs_2_, bf16[256,4096]{1,0:T(8,128)(2,1)} %close.6.refs_3_), custom_call_target="tpu_custom_call", output_to_operand_aliasing={{}: (3, {})} | custom-call | flops 1048576 | bytes 2097152 | tf_op jit(solution)/shard_map/close/pallas_call | solution.py:524
  75.5 1.0 %close.8.refs_3_ = bf16[256,4096]{1,0:T(8,128)(2,1)} custom-call(f32[8,256]{1,0:T(8,128)S(1)} %add_add_fusion.refs_0_, f32[256,768]{1,0:T(8,128)S(1)} %slice.12.refs_1_, bf16[256,768]{1,0:T(8,128)(2,1)S(1)} %collective-permute-done.15.refs_2_, bf16[256,4096]{1,0:T(8,128)(2,1)} %close.7.refs_3_), custom_call_target="tpu_custom_call", output_to_operand_aliasing={{}: (3, {})} | custom-call | flops 786432 | bytes 1572864 | tf_op jit(solution)/shard_map/close/pallas_call | solution.py:524
  76.5 6.2 %collective-permute-done.16.refs_2_ = bf16[256,768]{1,0:T(8,128)(2,1)S(1)} collective-permute-done((bf16[256,768]{1,0:T(8,128)(2,1)S(1)}, bf16[256,768]{1,0:T(8,128)(2,1)S(1)}, u32[]{:S(2)}, u32[]{:S(2)}) %collective-permute-start.16) | collective-permute-done | bytes 393248 | tf_op jit(solution)/shard_map/ppermute | solution.py:631
  82.8 1.0 %close.9.refs_3_ = bf16[256,4096]{1,0:T(8,128)(2,1)} custom-call(f32[8,256]{1,0:T(8,128)S(1)} %add_add_fusion.refs_0_, f32[256,768]{1,0:T(8,128)S(1)} %get-tuple-element.153.refs_1_, bf16[256,768]{1,0:T(8,128)(2,1)S(1)} %collective-permute-done.16.refs_2_, bf16[256,4096]{1,0:T(8,128)(2,1)} %close.8.refs_3_), custom_call_target="tpu_custom_call", output_to_operand_aliasing={{}: (3, {})} | custom-call | flops 786432 | bytes 1572864 | tf_op jit(solution)/shard_map/close/pallas_call | solution.py:524
  83.8 7.4 %collective-permute-done.17.refs_2_ = bf16[256,768]{1,0:T(8,128)(2,1)S(1)} collective-permute-done((bf16[256,768]{1,0:T(8,128)(2,1)S(1)}, bf16[256,768]{1,0:T(8,128)(2,1)S(1)}, u32[]{:S(2)}, u32[]{:S(2)}) %collective-permute-start.17) | collective-permute-done | bytes 393248 | tf_op jit(solution)/shard_map/ppermute | solution.py:631
  91.2 1.0 %close.10.refs_3_ = bf16[256,4096]{1,0:T(8,128)(2,1)} custom-call(f32[8,256]{1,0:T(8,128)S(1)} %add_add_fusion.refs_0_, f32[256,768]{1,0:T(8,128)S(1)} %get-tuple-element.152.refs_1_, bf16[256,768]{1,0:T(8,128)(2,1)S(1)} %collective-permute-done.17.refs_2_, bf16[256,4096]{1,0:T(8,128)(2,1)} %close.9.refs_3_), custom_call_target="tpu_custom_call", output_to_operand_aliasing={{}: (3, {})} | custom-call | flops 786432 | bytes 1572864 | tf_op jit(solution)/shard_map/close/pallas_call | solution.py:524
  92.3 0.9 collective-permute-done.18.refs_2_
  93.2 0.9 close.11
  (22 shorter events, 0.9 us)
Async XLA Ops:
  3.2 27.3 %collective-permute-start.10 = (bf16[1024,4096]{1,0:T(8,128)(2,1)}, bf16[1024,4096]{1,0:T(8,128)(2,1)S(1)}, u32[]{:S(2)}, u32[]{:S(2)}) collective-permute-start(bf16[1024,4096]{1,0:T(8,128)(2,1)} %refs_2_.5), channel_id=1, source_target_pairs={{0,1},{1,0},{2,3},{3,2},{4,5},{5,4},{6,7},{7,6},{8,9},{9,8},{10,11... | collective-permute-start | bytes 25165832 | tf_op jit(solution)/shard_map/ppermute | solution.py:575
  3.7 5.4 %collective-permute-start.1 = (bf16[2,136,128]{2,1,0:T(8,128)(2,1)S(1)}, bf16[2,136,128]{2,1,0:T(8,128)(2,1)S(1)}, u32[]{:S(2)}, u32[]{:S(2)}) collective-permute-start(bf16[2,136,128]{2,1,0:T(8,128)(2,1)S(1)} %get-tuple-element.101), channel_id=1, source_target_pairs={{0,8},{4,12},{8,0},{12,4},{16,24},{20,28},{24,16},{28,20},{1,9},{5... | collective-permute-start | bytes 208904 | tf_op jit(solution)/shard_map/ppermute | solution.py:565
  6.3 5.5 %collective-permute-start.2 = (bf16[2,136,128]{2,1,0:T(8,128)(2,1)S(1)}, bf16[2,136,128]{2,1,0:T(8,128)(2,1)S(1)}, u32[]{:S(2)}, u32[]{:S(2)}) collective-permute-start(bf16[2,136,128]{2,1,0:T(8,128)(2,1)S(1)} %get-tuple-element.102), channel_id=1, source_target_pairs={{0,12},{4,8},{8,4},{12,0},{16,28},{20,24},{24,20},{28,16},{1,13},{... | collective-permute-start | bytes 208904 | tf_op jit(solution)/shard_map/ppermute | solution.py:565
  7.7 5.3 %collective-permute-start = (bf16[2,136,128]{2,1,0:T(8,128)(2,1)S(1)}, bf16[2,136,128]{2,1,0:T(8,128)(2,1)S(1)}, u32[]{:S(2)}, u32[]{:S(2)}) collective-permute-start(bf16[2,136,128]{2,1,0:T(8,128)(2,1)S(1)} %get-tuple-element.88), channel_id=1, source_target_pairs={{0,4},{4,0},{8,12},{12,8},{16,20},{20,16},{24,28},{28,24},{1,5},{5... | collective-permute-start | bytes 208904 | tf_op jit(solution)/shard_map/ppermute | solution.py:565
  13.3 6.4 %collective-permute-start.3 = (bf16[2,136,128]{2,1,0:T(8,128)(2,1)S(1)}, bf16[2,136,128]{2,1,0:T(8,128)(2,1)S(1)}, u32[]{:S(2)}, u32[]{:S(2)}) collective-permute-start(bf16[2,136,128]{2,1,0:T(8,128)(2,1)S(1)} %get-tuple-element.103), channel_id=1, source_target_pairs={{0,16},{4,20},{8,24},{12,28},{16,0},{20,4},{24,8},{28,12},{1,17},{... | collective-permute-start | bytes 208904 | tf_op jit(solution)/shard_map/ppermute | solution.py:314
  19.8 6.5 %collective-permute-start.4 = (bf16[2,128,128]{2,1,0:T(8,128)(2,1)S(1)}, bf16[2,128,128]{2,1,0:T(8,128)(2,1)S(1)}, u32[]{:S(2)}, u32[]{:S(2)}) collective-permute-start(bf16[2,128,128]{2,1,0:T(8,128)(2,1)S(1)} %get-tuple-element.117), channel_id=1, source_target_pairs={{0,4},{4,0},{8,12},{12,8},{16,20},{20,16},{24,28},{28,24},{1,5},{5... | collective-permute-start | bytes 196616 | tf_op jit(solution)/shard_map/ppermute | solution.py:565
  20.5 5.8 %collective-permute-start.5 = (bf16[2,128,128]{2,1,0:T(8,128)(2,1)S(1)}, bf16[2,128,128]{2,1,0:T(8,128)(2,1)S(1)}, u32[]{:S(2)}, u32[]{:S(2)}) collective-permute-start(bf16[2,128,128]{2,1,0:T(8,128)(2,1)S(1)} %get-tuple-element.118), channel_id=1, source_target_pairs={{0,8},{4,12},{8,0},{12,4},{16,24},{20,28},{24,16},{28,20},{1,9},{5... | collective-permute-start | bytes 196616 | tf_op jit(solution)/shard_map/ppermute | solution.py:565
  20.7 5.6 %collective-permute-start.6 = (bf16[2,128,128]{2,1,0:T(8,128)(2,1)S(1)}, bf16[2,128,128]{2,1,0:T(8,128)(2,1)S(1)}, u32[]{:S(2)}, u32[]{:S(2)}) collective-permute-start(bf16[2,128,128]{2,1,0:T(8,128)(2,1)S(1)} %get-tuple-element.119), channel_id=1, source_target_pairs={{0,12},{4,8},{8,4},{12,0},{16,28},{20,24},{24,20},{28,16},{1,13},{... | collective-permute-start | bytes 196616 | tf_op jit(solution)/shard_map/ppermute | solution.py:565
  23.3 3.0 %copy-start = (f32[1024]{0:T(1024)S(1)}, f32[1024]{0:T(1024)}, u32[]{:S(2)}) copy-start(f32[1024]{0:T(1024)} %param.18) | copy-start | bytes 12292
  26.9 3.6 %collective-permute-start.9 = (bf16[256,1024]{1,0:T(8,128)(2,1)S(1)}, bf16[256,1024]{1,0:T(8,128)(2,1)S(1)}, u32[]{:S(2)}, u32[]{:S(2)}) collective-permute-start(bf16[256,1024]{1,0:T(8,128)(2,1)S(1)} %get-tuple-element.126), channel_id=1, source_target_pairs={{0,1},{1,0},{2,3},{3,2},{4,5},{5,4},{6,7},{7,6},{8,9},{9,8},{10,11... | collective-permute-start | bytes 1572872 | tf_op jit(solution)/shard_map/ppermute | solution.py:598
  41.9 9.6 %collective-permute-start.12 = (bf16[256,1024]{1,0:T(8,128)(2,1)S(1)}, bf16[256,1024]{1,0:T(8,128)(2,1)S(1)}, u32[]{:S(2)}, u32[]{:S(2)}) collective-permute-start(bf16[256,1024]{1,0:T(8,128)(2,1)S(1)} %get-tuple-element.142), channel_id=1, source_target_pairs={{0,1},{1,0},{2,3},{3,2},{4,5},{5,4},{6,7},{7,6},{8,9},{9,8},{10,11... | collective-permute-start | bytes 1572872 | tf_op jit(solution)/shard_map/ppermute | solution.py:598
  42.5 1.5 %collective-permute-start.7 = (f32[8,256]{1,0:T(8,128)S(1)}, f32[8,256]{1,0:T(8,128)S(1)}, u32[]{:S(2)}, u32[]{:S(2)}) collective-permute-start(f32[8,256]{1,0:T(8,128)S(1)} %get-tuple-element.124), channel_id=1, source_target_pairs={{0,1},{1,0},{2,3},{3,2},{4,5},{5,4},{6,7},{7,6},{8,9},{9,8},{10,11... | collective-permute-start | bytes 24584 | tf_op jit(solution)/shard_map/ppermute | solution.py:599
  44.0 14.9 %collective-permute-start.8 = (f32[8,256]{1,0:T(8,128)S(1)}, f32[8,256]{1,0:T(8,128)S(1)}, u32[]{:S(2)}, u32[]{:S(2)}) collective-permute-start(f32[8,256]{1,0:T(8,128)S(1)} %add.9), channel_id=1, source_target_pairs={{0,2},{1,3},{2,0},{3,1},{4,6},{5,7},{6,4},{7,5},{8,10},{9,11},{10,... | collective-permute-start | bytes 24584 | tf_op jit(solution)/shard_map/ppermute | solution.py:610
  45.5 30.0 %collective-permute-start.15 = (bf16[256,768]{1,0:T(8,128)(2,1)S(1)}, bf16[256,768]{1,0:T(8,128)(2,1)S(1)}, u32[]{:S(2)}, u32[]{:S(2)}) collective-permute-start(bf16[256,768]{1,0:T(8,128)(2,1)S(1)} %product.7), channel_id=1, source_target_pairs={{0,2},{1,3},{2,0},{3,1},{4,6},{5,7},{6,4},{7,5},{8,10},{9,11},{10,... | collective-permute-start | bytes 1179656 | tf_op jit(solution)/shard_map/ppermute | solution.py:631
  46.0 17.1 %collective-permute-start.13 = (bf16[256,512]{1,0:T(8,128)(2,1)S(1)}, bf16[256,512]{1,0:T(8,128)(2,1)S(1)}, u32[]{:S(2)}, u32[]{:S(2)}) collective-permute-start(bf16[256,512]{1,0:T(8,128)(2,1)S(1)} %first.1), channel_id=1, source_target_pairs={{0,2},{1,3},{2,0},{3,1},{4,6},{5,7},{6,4},{7,5},{8,10},{9,11},{10,... | collective-permute-start | bytes 786440 | tf_op jit(solution)/shard_map/ppermute | solution.py:631
  47.5 26.8 %collective-permute-start.14 = (bf16[256,1024]{1,0:T(8,128)(2,1)S(1)}, bf16[256,1024]{1,0:T(8,128)(2,1)S(1)}, u32[]{:S(2)}, u32[]{:S(2)}) collective-permute-start(bf16[256,1024]{1,0:T(8,128)(2,1)S(1)} %product.6), channel_id=1, source_target_pairs={{0,2},{1,3},{2,0},{3,1},{4,6},{5,7},{6,4},{7,5},{8,10},{9,11},{10,... | collective-permute-start | bytes 1572872 | tf_op jit(solution)/shard_map/ppermute | solution.py:631
  51.6 9.0 %collective-permute-start.11 = (f32[8,256]{1,0:T(8,128)S(1)}, f32[8,256]{1,0:T(8,128)S(1)}, u32[]{:S(2)}, u32[]{:S(2)}) collective-permute-start(f32[8,256]{1,0:T(8,128)S(1)} %get-tuple-element.139), channel_id=1, source_target_pairs={{0,1},{1,0},{2,3},{3,2},{4,5},{5,4},{6,7},{7,6},{8,9},{9,8},{10,11... | collective-permute-start | bytes 24584 | tf_op jit(solution)/shard_map/ppermute | solution.py:599
  58.9 23.9 %collective-permute-start.16 = (bf16[256,768]{1,0:T(8,128)(2,1)S(1)}, bf16[256,768]{1,0:T(8,128)(2,1)S(1)}, u32[]{:S(2)}, u32[]{:S(2)}) collective-permute-start(bf16[256,768]{1,0:T(8,128)(2,1)S(1)} %get-tuple-element.163), channel_id=1, source_target_pairs={{0,2},{1,3},{2,0},{3,1},{4,6},{5,7},{6,4},{7,5},{8,10},{9,11},{10,... | collective-permute-start | bytes 1179656 | tf_op jit(solution)/shard_map/ppermute | solution.py:631
  60.5 30.7 %collective-permute-start.17 = (bf16[256,768]{1,0:T(8,128)(2,1)S(1)}, bf16[256,768]{1,0:T(8,128)(2,1)S(1)}, u32[]{:S(2)}, u32[]{:S(2)}) collective-permute-start(bf16[256,768]{1,0:T(8,128)(2,1)S(1)} %get-tuple-element.166), channel_id=1, source_target_pairs={{0,2},{1,3},{2,0},{3,1},{4,6},{5,7},{6,4},{7,5},{8,10},{9,11},{10,... | collective-permute-start | bytes 1179656 | tf_op jit(solution)/shard_map/ppermute | solution.py:631
  63.1 30.0 %collective-permute-start.18 = (bf16[256,256]{1,0:T(8,128)(2,1)S(1)}, bf16[256,256]{1,0:T(8,128)(2,1)S(1)}, u32[]{:S(2)}, u32[]{:S(2)}) collective-permute-start(bf16[256,256]{1,0:T(8,128)(2,1)S(1)} %get-tuple-element.154), channel_id=1, source_target_pairs={{0,2},{1,3},{2,0},{3,1},{4,6},{5,7},{6,4},{7,5},{8,10},{9,11},{10,... | collective-permute-start | bytes 393224 | tf_op jit(solution)/shard_map/ppermute | solution.py:631

commit v2 on v1

--- a/solution.py
+++ b/solution.py
@@ -493,14 +493,30 @@
     )(a, b, wa, wb)
 
 
-def close(square, own, parts, inner, out, first, columns, shape, step=256):
+def factor(square, inner):
+    rows = square.shape[1]
+
+    def body(sq_ref, out_ref):
+        out_ref[...] = jnp.broadcast_to(lax.rsqrt(sq_ref[...] / inner + 1e-05).T[:, 0:1], (rows, LANES))
+
+    return pl.pallas_call(
+        body,
+        in_specs=[VECTORS],
+        out_specs=VECTORS,
+        out_shape=jax.ShapeDtypeStruct((rows, LANES), F32),
+        compiler_params=PARAMS,
+        name="factor",
+    )(square)
+
+
+def close(square, own, parts, out, first, columns, shape, step=256):
     rows = shape[0]
 
     def body(*refs):
         sq_ref, own_ref = refs[:2]
         part_refs = refs[2 : 2 + len(parts)]
         out_any, made_s, sems = refs[-3:]
-        row = lax.rsqrt(sq_ref[...] / inner + 1e-05).T[:, 0:1]
+        row = jnp.concatenate([sq_ref[...]] * (step // LANES), axis=1)
         copies = []
         for i in range(columns // step):
             here = slice(i * step, (i + 1) * step)
@@ -632,11 +648,11 @@
             last = after(direct, made[0])
     mine, _ = lax.optimization_barrier((mine, made[0]))
     early = product([mine], [F32], weight, weight_b, 0, places[ALONE], places[ALONE] // 3)[0]
-    square = sum(squares[1:], squares[0])
+    square = factor(sum(squares[1:], squares[0]), inner)
     out = None
     for c, n in enumerate(CUTS):
         own = early[:, places[c] : places[c + 1]] if c < ALONE else owns[c]
-        out = close(square, own, received[c], inner, out, places[c], n * unit, (SPAN, out_columns))
+        out = close(square, own, received[c], out, places[c], n * unit, (SPAN, out_columns))
         if c + 1 < len(CUTS):
             out, received[c + 1] = lax.optimization_barrier((out, received[c + 1]))
     return out

time: 94.8 us -> 94.1 us (level)
  Pallas kernels: 46.4 us -> 45.2 us
    pallas_call x6, Pallas kernels: 6.15 us -> 4.75 us  [close(): pl.pallas_call(body, in_specs=in_specs, out_specs=ANYWHERE, out_shape=jax...]
  transfers between devices with their start and end apart: 19 -> 19, of which waited for: 10 -> 10; matrix products, arithmetic and copies ran while one was open for 0% -> 0% of each run, Pallas kernels for 33% -> 32%
where the time goes in v2:
time: 94.1 us; the launch traced here: 93.6 us
  Pallas kernels  45.2 us (48%)
  waiting for transfers between devices  28.4 us (30%)
  starting transfers between devices  19.3 us (21%)
    pallas_call x6, Pallas kernels, product(): pl.pallas_call(functools.partial(product_kernel, count=count), grid=(colu...  20.6 us
    ppermute x6, waiting for transfers between devices, local(): received[c].append(lax.ppermute(made[0], 'head', send))  19.4 us
    pallas_call x4, Pallas kernels, intra(): pl.pallas_call(functools.partial(intra_kernel, k=k, teams=teams, which=wh...  11.7 us
    ppermute x6, starting transfers between devices, around(): lax.ppermute(items[k], 'seq', [(i, i ^ k) for i in range(shards)])  7.67 us
    ppermute x6, starting transfers between devices, local(): received[c].append(lax.ppermute(made[0], 'head', send))  6.18 us
    pallas_call x6, Pallas kernels, close(): pl.pallas_call(body, in_specs=in_specs, out_specs=ANYWHERE, out_shape=jax...  4.75 us
    ppermute x6, waiting for transfers between devices, around(): lax.ppermute(items[k], 'seq', [(i, i ^ k) for i in range(shards)])  4.17 us
    ppermute x1, waiting for transfers between devices, across(): lax.ppermute(send, 'seq', [(i, i ^ RING * level) for i in range(shards)])  3.36 us
  transfers between devices with their start and end apart: 19, of which 10 were waited for; matrix products, arithmetic and copies ran while one was open for 0% of the time, Pallas kernels for 32%

profile of v2, /device:TPU:0, one launch (start us, length us, event | category | flops | bytes accessed | tf_op | source)
XLA Modules:
  0.0 93.6 jit_solution(12537910510180409188)
XLA Ops:
  0.0 3.1 %states.1 = (bf16[2,136,128]{2,1,0:T(8,128)(2,1)S(1)}, bf16[2,136,128]{2,1,0:T(8,128)(2,1)S(1)}, bf16[2,136,128]{2,1,0:T(8,128)(2,1)S(1)}, bf16[4,128,1024]{2,1,...) custom-call(f32[1,16]{1,0:T(1,128)} %bitcast.9, ...), custom_call_target="tpu_custom_call" | custom-call | flops 402653184 | bytes 4194304 | tf_op jit(solution)/shard_map/states/pallas_call | solution.py:185
  3.2 0.6 collective-permute-start.10
  3.7 2.6 %collective-permute-start = (bf16[2,136,128]{2,1,0:T(8,128)(2,1)S(1)}, bf16[2,136,128]{2,1,0:T(8,128)(2,1)S(1)}, u32[]{:S(2)}, u32[]{:S(2)}) collective-permute-start(bf16[2,136,128]{2,1,0:T(8,128)(2,1)S(1)} %get-tuple-element.88), channel_id=1, source_target_pairs={{0,4},{4,0},{8,12},{12,8},{16,20},{20,16},{24,28},{28,24},{1,5},{5... | collective-permute-start | bytes 208904 | tf_op jit(solution)/shard_map/ppermute | solution.py:581
  6.3 1.6 %collective-permute-start.1 = (bf16[2,136,128]{2,1,0:T(8,128)(2,1)S(1)}, bf16[2,136,128]{2,1,0:T(8,128)(2,1)S(1)}, u32[]{:S(2)}, u32[]{:S(2)}) collective-permute-start(bf16[2,136,128]{2,1,0:T(8,128)(2,1)S(1)} %get-tuple-element.101), channel_id=1, source_target_pairs={{0,8},{4,12},{8,0},{12,4},{16,24},{20,28},{24,16},{28,20},{1,9},{5... | collective-permute-start | bytes 208904 | tf_op jit(solution)/shard_map/ppermute | solution.py:581
  7.8 1.0 %tables.1 = (bf16[2,136,128]{2,1,0:T(8,128)(2,1)S(1)}, bf16[4,128,1024]{2,1,0:T(8,128)(2,1)S(1)}, f32[4,8,1024]{2,1,0:T(8,128)S(1)}, f32[16,1024]{1,0:T(8,128)S(...) custom-call(f32[1,16]{1,0:T(1,128)} %bitcast.10, ...), custom_call_target="tpu_custom_call", output_to_operand_aliasing={{1}: (1, {}), {2}: (2, {})} | custom-call | flops 134217728 | bytes 4194304 | tf_op jit(solution)/shard_map/tables/pallas_call | solution.py:221
  8.9 0.2 collective-permute-done.refs_1_
  9.0 1.8 %collective-permute-done.1.refs_2_ = bf16[2,136,128]{2,1,0:T(8,128)(2,1)S(1)} collective-permute-done((bf16[2,136,128]{2,1,0:T(8,128)(2,1)S(1)}, bf16[2,136,128]{2,1,0:T(8,128)(2,1)S(1)}, u32[]{:S(2)}, u32[]{:S(2)}) %collective-permute-start.1) | collective-permute-done | bytes 69664 | tf_op jit(solution)/shard_map/ppermute | solution.py:581
  10.9 2.2 %collective-permute-done.2.refs_3_ = bf16[2,136,128]{2,1,0:T(8,128)(2,1)S(1)} collective-permute-done((bf16[2,136,128]{2,1,0:T(8,128)(2,1)S(1)}, bf16[2,136,128]{2,1,0:T(8,128)(2,1)S(1)}, u32[]{:S(2)}, u32[]{:S(2)}) %collective-permute-start.2) | collective-permute-done | bytes 69664 | tf_op jit(solution)/shard_map/ppermute | solution.py:581
  13.0 0.2 prefix.1
  13.2 2.7 %collective-permute-start.3 = (bf16[2,136,128]{2,1,0:T(8,128)(2,1)S(1)}, bf16[2,136,128]{2,1,0:T(8,128)(2,1)S(1)}, u32[]{:S(2)}, u32[]{:S(2)}) collective-permute-start(bf16[2,136,128]{2,1,0:T(8,128)(2,1)S(1)} %get-tuple-element.103), channel_id=1, source_target_pairs={{0,16},{4,20},{8,24},{12,28},{16,0},{20,4},{24,8},{28,12},{1,17},{... | collective-permute-start | bytes 208904 | tf_op jit(solution)/shard_map/ppermute | solution.py:314
  15.9 3.4 %collective-permute-done.3.left_ref = bf16[2,136,128]{2,1,0:T(8,128)(2,1)S(1)} collective-permute-done((bf16[2,136,128]{2,1,0:T(8,128)(2,1)S(1)}, bf16[2,136,128]{2,1,0:T(8,128)(2,1)S(1)}, u32[]{:S(2)}, u32[]{:S(2)}) %collective-permute-start.3) | collective-permute-done | bytes 69664 | tf_op jit(solution)/shard_map/ppermute | solution.py:314
  19.4 1.2 %collective-permute-start.5 = (bf16[2,128,128]{2,1,0:T(8,128)(2,1)S(1)}, bf16[2,128,128]{2,1,0:T(8,128)(2,1)S(1)}, u32[]{:S(2)}, u32[]{:S(2)}) collective-permute-start(bf16[2,128,128]{2,1,0:T(8,128)(2,1)S(1)} %get-tuple-element.118), channel_id=1, source_target_pairs={{0,8},{4,12},{8,0},{12,4},{16,24},{20,28},{24,16},{28,20},{1,9},{5... | collective-permute-start | bytes 196616 | tf_op jit(solution)/shard_map/ppermute | solution.py:581
  20.6 2.3 %collective-permute-start.6 = (bf16[2,128,128]{2,1,0:T(8,128)(2,1)S(1)}, bf16[2,128,128]{2,1,0:T(8,128)(2,1)S(1)}, u32[]{:S(2)}, u32[]{:S(2)}) collective-permute-start(bf16[2,128,128]{2,1,0:T(8,128)(2,1)S(1)} %get-tuple-element.119), channel_id=1, source_target_pairs={{0,12},{4,8},{8,4},{12,0},{16,28},{20,24},{24,20},{28,16},{1,13},{... | collective-permute-start | bytes 196616 | tf_op jit(solution)/shard_map/ppermute | solution.py:581
  22.9 2.9 %intra.5 = (f32[256,1024]{1,0:T(8,128)S(1)}, bf16[256,1024]{1,0:T(8,128)(2,1)S(1)}) custom-call(f32[16,128]{1,0:T(8,128)S(1)} %get-tuple-element.132.skip_ref, bf16[1024,128]{1,0:T(8,128)(2,1)S(1)} %get-tuple-element.108.b_ref, bf16[1024,128]{1,0:T(8,128)(2,1)S(1)} %get-tuple-element.109.c_ref, f32[16,1024]{1,0:T(8,128)S(1)} %get-tuple-element.110.row_ref, ...), custom_call_target="tpu_custom_call" | custom-call | flops 536870912 | bytes 2097152 | tf_op jit(solution)/shard_map/intra/pallas_call | solution.py:385
  25.9 0.6 finish.5
  26.5 2.9 %intra.4 = (f32[256,1024]{1,0:T(8,128)S(1)}, bf16[256,1024]{1,0:T(8,128)(2,1)S(1)}, bf16[1024,512]{1,0:T(8,128)(2,1)S(1)}) custom-call(f32[16,128]{1,0:T(8,128)S(1)} %get-tuple-element.132.skip_ref, bf16[1024,128]{1,0:T(8,128)(2,1)S(1)} %get-tuple-element.108.b_ref, bf16[1024,128]{1,0:T(8,128)(2,1)S(1)} %get-tuple-element.109.c_ref, ...), custom_call_target="tpu_custom_call" | custom-call | flops 536870912 | bytes 2097152 | tf_op jit(solution)/shard_map/intra/pallas_call | solution.py:385
  29.5 0.6 finish.4
  30.0 1.2 %first.1 = bf16[256,512]{1,0:T(8,128)(2,1)S(1)} custom-call(bf16[256,1024]{1,0:T(8,128)(2,1)S(1)} %get-tuple-element.148.a_ref.refs_0_, bf16[256,1024]{1,0:T(8,128)(2,1)S(1)} %collective-permute-done.9.b_ref.refs_1_, bf16[1024,512]{1,0:T(8,128)(2,1)S(1)} %get-tuple-element.127.wa_ref, bf16[1024,4096]{1,0:T(8,128)(2,1)S(1)} %collective-permute-done.10.wb_any.refs_3_.refs_5_), custom_call_target="tpu_custom_call" | custom-call | flops 536870912 | bytes 2097152 | tf_op jit(solution)/shard_map/first/pallas_call | solution.py:484
  31.3 3.6 %product.6 = bf16[256,1024]{1,0:T(8,128)(2,1)S(1)} custom-call(bf16[256,1024]{1,0:T(8,128)(2,1)S(1)} %get-tuple-element.148.a_ref.refs_0_, bf16[256,1024]{1,0:T(8,128)(2,1)S(1)} %collective-permute-done.9.b_ref.refs_1_, bf16[1024,4096]{1,0:T(8,128)(2,1)} %refs_2_.5, bf16[1024,4096]{1,0:T(8,128)(2,1)S(1)} %collective-permute-done.10.wb_any.refs_3_.refs_5_), custom_call_target="tpu_custom_call" | custom-call | flops 1073741824 | bytes 4194304 | tf_op jit(solution)/shard_map/product/pallas_call | solution.py:456
  34.9 3.0 %product.7 = bf16[256,768]{1,0:T(8,128)(2,1)S(1)} custom-call(bf16[256,1024]{1,0:T(8,128)(2,1)S(1)} %get-tuple-element.148.a_ref.refs_0_, bf16[256,1024]{1,0:T(8,128)(2,1)S(1)} %collective-permute-done.9.b_ref.refs_1_, bf16[1024,4096]{1,0:T(8,128)(2,1)} %refs_2_.5, bf16[1024,4096]{1,0:T(8,128)(2,1)S(1)} %collective-permute-done.10.wb_any.refs_3_.refs_5_), custom_call_target="tpu_custom_call" | custom-call | flops 805306368 | bytes 3145728 | tf_op jit(solution)/shard_map/product/pallas_call | solution.py:456
  38.0 2.9 %intra.7 = (f32[256,1024]{1,0:T(8,128)S(1)}, bf16[256,1024]{1,0:T(8,128)(2,1)S(1)}) custom-call(f32[16,128]{1,0:T(8,128)S(1)} %get-tuple-element.132.skip_ref, bf16[1024,128]{1,0:T(8,128)(2,1)S(1)} %get-tuple-element.108.b_ref, bf16[1024,128]{1,0:T(8,128)(2,1)S(1)} %get-tuple-element.109.c_ref, f32[16,1024]{1,0:T(8,128)S(1)} %get-tuple-element.110.row_ref, ...), custom_call_target="tpu_custom_call" | custom-call | flops 536870912 | bytes 2097152 | tf_op jit(solution)/shard_map/intra/pallas_call | solution.py:385
  40.9 0.6 finish.7
  41.5 0.5 collective-permute-start.12
  42.1 1.5 %collective-permute-done.7 = f32[8,256]{1,0:T(8,128)S(1)} collective-permute-done((f32[8,256]{1,0:T(8,128)S(1)}, f32[8,256]{1,0:T(8,128)S(1)}, u32[]{:S(2)}, u32[]{:S(2)}) %collective-permute-start.7) | collective-permute-done | bytes 8224 | tf_op jit(solution)/shard_map/ppermute | solution.py:615
  43.6 1.5 %collective-permute-start.8 = (f32[8,256]{1,0:T(8,128)S(1)}, f32[8,256]{1,0:T(8,128)S(1)}, u32[]{:S(2)}, u32[]{:S(2)}) collective-permute-start(f32[8,256]{1,0:T(8,128)S(1)} %add.9), channel_id=1, source_target_pairs={{0,2},{1,3},{2,0},{3,1},{4,6},{5,7},{6,4},{7,5},{8,10},{9,11},{10,... | collective-permute-start | bytes 24584 | tf_op jit(solution)/shard_map/ppermute | solution.py:626
  45.1 0.5 collective-permute-start.15
  45.6 1.5 %collective-permute-start.13 = (bf16[256,512]{1,0:T(8,128)(2,1)S(1)}, bf16[256,512]{1,0:T(8,128)(2,1)S(1)}, u32[]{:S(2)}, u32[]{:S(2)}) collective-permute-start(bf16[256,512]{1,0:T(8,128)(2,1)S(1)} %first.1), channel_id=1, source_target_pairs={{0,2},{1,3},{2,0},{3,1},{4,6},{5,7},{6,4},{7,5},{8,10},{9,11},{10,... | collective-permute-start | bytes 786440 | tf_op jit(solution)/shard_map/ppermute | solution.py:647
  47.1 2.9 %intra.6 = (f32[256,1024]{1,0:T(8,128)S(1)}, bf16[256,1024]{1,0:T(8,128)(2,1)S(1)}) custom-call(f32[16,128]{1,0:T(8,128)S(1)} %get-tuple-element.132.skip_ref, bf16[1024,128]{1,0:T(8,128)(2,1)S(1)} %get-tuple-element.108.b_ref, bf16[1024,128]{1,0:T(8,128)(2,1)S(1)} %get-tuple-element.109.c_ref, f32[16,1024]{1,0:T(8,128)S(1)} %get-tuple-element.110.row_ref, ...), custom_call_target="tpu_custom_call" | custom-call | flops 536870912 | bytes 2097152 | tf_op jit(solution)/shard_map/intra/pallas_call | solution.py:385
  50.0 0.6 finish.6
  50.6 0.6 collective-permute-start.14
  51.2 3.6 %product.8 = (bf16[256,768]{1,0:T(8,128)(2,1)S(1)}, f32[256,768]{1,0:T(8,128)S(1)}) custom-call(bf16[256,1024]{1,0:T(8,128)(2,1)S(1)} %get-tuple-element.148.a_ref.refs_0_, bf16[256,1024]{1,0:T(8,128)(2,1)S(1)} %collective-permute-done.9.b_ref.refs_1_, bf16[256,1024]{1,0:T(8,128)(2,1)S(1)} %get-tuple-element.155.refs_2_.refs_0_, ...), custom_call_target="tpu_custom_call" | custom-call | flops 1610612736 | bytes 3145728 | tf_op jit(solution)/shard_map/product/pallas_call | solution.py:456
  54.8 3.6 %product.9 = (bf16[256,768]{1,0:T(8,128)(2,1)S(1)}, f32[256,768]{1,0:T(8,128)S(1)}) custom-call(bf16[256,1024]{1,0:T(8,128)(2,1)S(1)} %get-tuple-element.148.a_ref.refs_0_, bf16[256,1024]{1,0:T(8,128)(2,1)S(1)} %collective-permute-done.9.b_ref.refs_1_, bf16[256,1024]{1,0:T(8,128)(2,1)S(1)} %get-tuple-element.155.refs_2_.refs_0_, ...), custom_call_target="tpu_custom_call" | custom-call | flops 1610612736 | bytes 3145728 | tf_op jit(solution)/shard_map/product/pallas_call | solution.py:456
  58.5 1.6 %collective-permute-start.16 = (bf16[256,768]{1,0:T(8,128)(2,1)S(1)}, bf16[256,768]{1,0:T(8,128)(2,1)S(1)}, u32[]{:S(2)}, u32[]{:S(2)}) collective-permute-start(bf16[256,768]{1,0:T(8,128)(2,1)S(1)} %get-tuple-element.163), channel_id=1, source_target_pairs={{0,2},{1,3},{2,0},{3,1},{4,6},{5,7},{6,4},{7,5},{8,10},{9,11},{10,... | collective-permute-start | bytes 1179656 | tf_op jit(solution)/shard_map/ppermute | solution.py:647
  60.1 0.5 collective-permute-start.17
  60.6 0.2 factor.1.refs_0_
  60.8 1.8 %product.10 = (bf16[256,256]{1,0:T(8,128)(2,1)S(1)}, f32[256,256]{1,0:T(8,128)S(1)}) custom-call(bf16[256,1024]{1,0:T(8,128)(2,1)S(1)} %get-tuple-element.148.a_ref.refs_0_, bf16[256,1024]{1,0:T(8,128)(2,1)S(1)} %collective-permute-done.9.b_ref.refs_1_, bf16[256,1024]{1,0:T(8,128)(2,1)S(1)} %get-tuple-element.155.refs_2_.refs_0_, ...), custom_call_target="tpu_custom_call" | custom-call | flops 536870912 | bytes 1048576 | tf_op jit(solution)/shard_map/product/pallas_call | solution.py:456
  62.7 1.5 %collective-permute-start.18 = (bf16[256,256]{1,0:T(8,128)(2,1)S(1)}, bf16[256,256]{1,0:T(8,128)(2,1)S(1)}, u32[]{:S(2)}, u32[]{:S(2)}) collective-permute-start(bf16[256,256]{1,0:T(8,128)(2,1)S(1)} %get-tuple-element.154), channel_id=1, source_target_pairs={{0,2},{1,3},{2,0},{3,1},{4,6},{5,7},{6,4},{7,5},{8,10},{9,11},{10,... | collective-permute-start | bytes 393224 | tf_op jit(solution)/shard_map/ppermute | solution.py:647
  64.2 4.9 %product.11 = f32[256,2304]{1,0:T(8,128)S(1)} custom-call(bf16[256,1024]{1,0:T(8,128)(2,1)S(1)} %get-tuple-element.155.refs_2_.refs_0_, bf16[256,1024]{1,0:T(8,128)(2,1)S(1)} %collective-permute-done.12.refs_3_.refs_1_, bf16[1024,4096]{1,0:T(8,128)(2,1)} %refs_2_.5, bf16[1024,4096]{1,0:T(8,128)(2,1)S(1)} %collective-permute-done.10.wb_any.refs_3_.refs_5_), custom_call_target="tpu_custom_call" | custom-call | flops 2415919104 | bytes 9437184 | tf_op jit(solution)/shard_map/product/pallas_call | solution.py:456
  69.3 0.8 close.6.refs_3_
  70.1 3.8 %collective-permute-done.14.refs_2_ = bf16[256,1024]{1,0:T(8,128)(2,1)S(1)} collective-permute-done((bf16[256,1024]{1,0:T(8,128)(2,1)S(1)}, bf16[256,1024]{1,0:T(8,128)(2,1)S(1)}, u32[]{:S(2)}, u32[]{:S(2)}) %collective-permute-start.14) | collective-permute-done | bytes 524320 | tf_op jit(solution)/shard_map/ppermute | solution.py:647
  73.9 0.9 close.7.refs_3_
  74.8 0.8 close.8.refs_3_
  75.6 6.7 %collective-permute-done.16.refs_2_ = bf16[256,768]{1,0:T(8,128)(2,1)S(1)} collective-permute-done((bf16[256,768]{1,0:T(8,128)(2,1)S(1)}, bf16[256,768]{1,0:T(8,128)(2,1)S(1)}, u32[]{:S(2)}, u32[]{:S(2)}) %collective-permute-start.16) | collective-permute-done | bytes 393248 | tf_op jit(solution)/shard_map/ppermute | solution.py:647
  82.4 0.8 close.9.refs_3_
  83.2 7.6 %collective-permute-done.17.refs_2_ = bf16[256,768]{1,0:T(8,128)(2,1)S(1)} collective-permute-done((bf16[256,768]{1,0:T(8,128)(2,1)S(1)}, bf16[256,768]{1,0:T(8,128)(2,1)S(1)}, u32[]{:S(2)}, u32[]{:S(2)}) %collective-permute-start.17) | collective-permute-done | bytes 393248 | tf_op jit(solution)/shard_map/ppermute | solution.py:647
  90.8 0.8 close.10.refs_3_
  91.6 1.1 %collective-permute-done.18.refs_2_ = bf16[256,256]{1,0:T(8,128)(2,1)S(1)} collective-permute-done((bf16[256,256]{1,0:T(8,128)(2,1)S(1)}, bf16[256,256]{1,0:T(8,128)(2,1)S(1)}, u32[]{:S(2)}, u32[]{:S(2)}) %collective-permute-start.18) | collective-permute-done | bytes 131104 | tf_op jit(solution)/shard_map/ppermute | solution.py:647
  92.7 0.7 close.11
  (23 shorter events, 0.7 us)
Async XLA Ops:
  3.2 26.9 %collective-permute-start.10 = (bf16[1024,4096]{1,0:T(8,128)(2,1)}, bf16[1024,4096]{1,0:T(8,128)(2,1)S(1)}, u32[]{:S(2)}, u32[]{:S(2)}) collective-permute-start(bf16[1024,4096]{1,0:T(8,128)(2,1)} %refs_2_.5), channel_id=1, source_target_pairs={{0,1},{1,0},{2,3},{3,2},{4,5},{5,4},{6,7},{7,6},{8,9},{9,8},{10,11... | collective-permute-start | bytes 25165832 | tf_op jit(solution)/shard_map/ppermute | solution.py:591
  3.7 5.3 %collective-permute-start = (bf16[2,136,128]{2,1,0:T(8,128)(2,1)S(1)}, bf16[2,136,128]{2,1,0:T(8,128)(2,1)S(1)}, u32[]{:S(2)}, u32[]{:S(2)}) collective-permute-start(bf16[2,136,128]{2,1,0:T(8,128)(2,1)S(1)} %get-tuple-element.88), channel_id=1, source_target_pairs={{0,4},{4,0},{8,12},{12,8},{16,20},{20,16},{24,28},{28,24},{1,5},{5... | collective-permute-start | bytes 208904 | tf_op jit(solution)/shard_map/ppermute | solution.py:581
  6.3 4.6 %collective-permute-start.1 = (bf16[2,136,128]{2,1,0:T(8,128)(2,1)S(1)}, bf16[2,136,128]{2,1,0:T(8,128)(2,1)S(1)}, u32[]{:S(2)}, u32[]{:S(2)}) collective-permute-start(bf16[2,136,128]{2,1,0:T(8,128)(2,1)S(1)} %get-tuple-element.101), channel_id=1, source_target_pairs={{0,8},{4,12},{8,0},{12,4},{16,24},{20,28},{24,16},{28,20},{1,9},{5... | collective-permute-start | bytes 208904 | tf_op jit(solution)/shard_map/ppermute | solution.py:581
  7.8 5.2 %collective-permute-start.2 = (bf16[2,136,128]{2,1,0:T(8,128)(2,1)S(1)}, bf16[2,136,128]{2,1,0:T(8,128)(2,1)S(1)}, u32[]{:S(2)}, u32[]{:S(2)}) collective-permute-start(bf16[2,136,128]{2,1,0:T(8,128)(2,1)S(1)} %get-tuple-element.102), channel_id=1, source_target_pairs={{0,12},{4,8},{8,4},{12,0},{16,28},{20,24},{24,20},{28,16},{1,13},{... | collective-permute-start | bytes 208904 | tf_op jit(solution)/shard_map/ppermute | solution.py:581
  13.2 6.0 %collective-permute-start.3 = (bf16[2,136,128]{2,1,0:T(8,128)(2,1)S(1)}, bf16[2,136,128]{2,1,0:T(8,128)(2,1)S(1)}, u32[]{:S(2)}, u32[]{:S(2)}) collective-permute-start(bf16[2,136,128]{2,1,0:T(8,128)(2,1)S(1)} %get-tuple-element.103), channel_id=1, source_target_pairs={{0,16},{4,20},{8,24},{12,28},{16,0},{20,4},{24,8},{28,12},{1,17},{... | collective-permute-start | bytes 208904 | tf_op jit(solution)/shard_map/ppermute | solution.py:314
  19.3 6.5 %collective-permute-start.4 = (bf16[2,128,128]{2,1,0:T(8,128)(2,1)S(1)}, bf16[2,128,128]{2,1,0:T(8,128)(2,1)S(1)}, u32[]{:S(2)}, u32[]{:S(2)}) collective-permute-start(bf16[2,128,128]{2,1,0:T(8,128)(2,1)S(1)} %get-tuple-element.117), channel_id=1, source_target_pairs={{0,4},{4,0},{8,12},{12,8},{16,20},{20,16},{24,28},{28,24},{1,5},{5... | collective-permute-start | bytes 196616 | tf_op jit(solution)/shard_map/ppermute | solution.py:581
  19.4 6.4 %collective-permute-start.5 = (bf16[2,128,128]{2,1,0:T(8,128)(2,1)S(1)}, bf16[2,128,128]{2,1,0:T(8,128)(2,1)S(1)}, u32[]{:S(2)}, u32[]{:S(2)}) collective-permute-start(bf16[2,128,128]{2,1,0:T(8,128)(2,1)S(1)} %get-tuple-element.118), channel_id=1, source_target_pairs={{0,8},{4,12},{8,0},{12,4},{16,24},{20,28},{24,16},{28,20},{1,9},{5... | collective-permute-start | bytes 196616 | tf_op jit(solution)/shard_map/ppermute | solution.py:581
  20.6 5.2 %collective-permute-start.6 = (bf16[2,128,128]{2,1,0:T(8,128)(2,1)S(1)}, bf16[2,128,128]{2,1,0:T(8,128)(2,1)S(1)}, u32[]{:S(2)}, u32[]{:S(2)}) collective-permute-start(bf16[2,128,128]{2,1,0:T(8,128)(2,1)S(1)} %get-tuple-element.119), channel_id=1, source_target_pairs={{0,12},{4,8},{8,4},{12,0},{16,28},{20,24},{24,20},{28,16},{1,13},{... | collective-permute-start | bytes 196616 | tf_op jit(solution)/shard_map/ppermute | solution.py:581
  22.9 3.0 %copy-start = (f32[1024]{0:T(1024)S(1)}, f32[1024]{0:T(1024)}, u32[]{:S(2)}) copy-start(f32[1024]{0:T(1024)} %param.18) | copy-start | bytes 12292
  26.4 3.6 %collective-permute-start.9 = (bf16[256,1024]{1,0:T(8,128)(2,1)S(1)}, bf16[256,1024]{1,0:T(8,128)(2,1)S(1)}, u32[]{:S(2)}, u32[]{:S(2)}) collective-permute-start(bf16[256,1024]{1,0:T(8,128)(2,1)S(1)} %get-tuple-element.126), channel_id=1, source_target_pairs={{0,1},{1,0},{2,3},{3,2},{4,5},{5,4},{6,7},{7,6},{8,9},{9,8},{10,11... | collective-permute-start | bytes 1572872 | tf_op jit(solution)/shard_map/ppermute | solution.py:614
  41.5 9.1 %collective-permute-start.12 = (bf16[256,1024]{1,0:T(8,128)(2,1)S(1)}, bf16[256,1024]{1,0:T(8,128)(2,1)S(1)}, u32[]{:S(2)}, u32[]{:S(2)}) collective-permute-start(bf16[256,1024]{1,0:T(8,128)(2,1)S(1)} %get-tuple-element.142), channel_id=1, source_target_pairs={{0,1},{1,0},{2,3},{3,2},{4,5},{5,4},{6,7},{7,6},{8,9},{9,8},{10,11... | collective-permute-start | bytes 1572872 | tf_op jit(solution)/shard_map/ppermute | solution.py:614
  42.0 1.5 %collective-permute-start.7 = (f32[8,256]{1,0:T(8,128)S(1)}, f32[8,256]{1,0:T(8,128)S(1)}, u32[]{:S(2)}, u32[]{:S(2)}) collective-permute-start(f32[8,256]{1,0:T(8,128)S(1)} %get-tuple-element.124), channel_id=1, source_target_pairs={{0,1},{1,0},{2,3},{3,2},{4,5},{5,4},{6,7},{7,6},{8,9},{9,8},{10,11... | collective-permute-start | bytes 24584 | tf_op jit(solution)/shard_map/ppermute | solution.py:615
  43.6 14.9 %collective-permute-start.8 = (f32[8,256]{1,0:T(8,128)S(1)}, f32[8,256]{1,0:T(8,128)S(1)}, u32[]{:S(2)}, u32[]{:S(2)}) collective-permute-start(f32[8,256]{1,0:T(8,128)S(1)} %add.9), channel_id=1, source_target_pairs={{0,2},{1,3},{2,0},{3,1},{4,6},{5,7},{6,4},{7,5},{8,10},{9,11},{10,... | collective-permute-start | bytes 24584 | tf_op jit(solution)/shard_map/ppermute | solution.py:626
  45.1 29.7 %collective-permute-start.15 = (bf16[256,768]{1,0:T(8,128)(2,1)S(1)}, bf16[256,768]{1,0:T(8,128)(2,1)S(1)}, u32[]{:S(2)}, u32[]{:S(2)}) collective-permute-start(bf16[256,768]{1,0:T(8,128)(2,1)S(1)} %product.7), channel_id=1, source_target_pairs={{0,2},{1,3},{2,0},{3,1},{4,6},{5,7},{6,4},{7,5},{8,10},{9,11},{10,... | collective-permute-start | bytes 1179656 | tf_op jit(solution)/shard_map/ppermute | solution.py:647
  45.6 14.5 %collective-permute-start.11 = (f32[8,256]{1,0:T(8,128)S(1)}, f32[8,256]{1,0:T(8,128)S(1)}, u32[]{:S(2)}, u32[]{:S(2)}) collective-permute-start(f32[8,256]{1,0:T(8,128)S(1)} %get-tuple-element.139), channel_id=1, source_target_pairs={{0,1},{1,0},{2,3},{3,2},{4,5},{5,4},{6,7},{7,6},{8,9},{9,8},{10,11... | collective-permute-start | bytes 24584 | tf_op jit(solution)/shard_map/ppermute | solution.py:615
  45.6 17.1 %collective-permute-start.13 = (bf16[256,512]{1,0:T(8,128)(2,1)S(1)}, bf16[256,512]{1,0:T(8,128)(2,1)S(1)}, u32[]{:S(2)}, u32[]{:S(2)}) collective-permute-start(bf16[256,512]{1,0:T(8,128)(2,1)S(1)} %first.1), channel_id=1, source_target_pairs={{0,2},{1,3},{2,0},{3,1},{4,6},{5,7},{6,4},{7,5},{8,10},{9,11},{10,... | collective-permute-start | bytes 786440 | tf_op jit(solution)/shard_map/ppermute | solution.py:647
  50.6 23.3 %collective-permute-start.14 = (bf16[256,1024]{1,0:T(8,128)(2,1)S(1)}, bf16[256,1024]{1,0:T(8,128)(2,1)S(1)}, u32[]{:S(2)}, u32[]{:S(2)}) collective-permute-start(bf16[256,1024]{1,0:T(8,128)(2,1)S(1)} %product.6), channel_id=1, source_target_pairs={{0,2},{1,3},{2,0},{3,1},{4,6},{5,7},{6,4},{7,5},{8,10},{9,11},{10,... | collective-permute-start | bytes 1572872 | tf_op jit(solution)/shard_map/ppermute | solution.py:647
  58.5 23.9 %collective-permute-start.16 = (bf16[256,768]{1,0:T(8,128)(2,1)S(1)}, bf16[256,768]{1,0:T(8,128)(2,1)S(1)}, u32[]{:S(2)}, u32[]{:S(2)}) collective-permute-start(bf16[256,768]{1,0:T(8,128)(2,1)S(1)} %get-tuple-element.163), channel_id=1, source_target_pairs={{0,2},{1,3},{2,0},{3,1},{4,6},{5,7},{6,4},{7,5},{8,10},{9,11},{10,... | collective-permute-start | bytes 1179656 | tf_op jit(solution)/shard_map/ppermute | solution.py:647
  60.1 30.7 %collective-permute-start.17 = (bf16[256,768]{1,0:T(8,128)(2,1)S(1)}, bf16[256,768]{1,0:T(8,128)(2,1)S(1)}, u32[]{:S(2)}, u32[]{:S(2)}) collective-permute-start(bf16[256,768]{1,0:T(8,128)(2,1)S(1)} %get-tuple-element.166), channel_id=1, source_target_pairs={{0,2},{1,3},{2,0},{3,1},{4,6},{5,7},{6,4},{7,5},{8,10},{9,11},{10,... | collective-permute-start | bytes 1179656 | tf_op jit(solution)/shard_map/ppermute | solution.py:647
  62.7 30.0 %collective-permute-start.18 = (bf16[256,256]{1,0:T(8,128)(2,1)S(1)}, bf16[256,256]{1,0:T(8,128)(2,1)S(1)}, u32[]{:S(2)}, u32[]{:S(2)}) collective-permute-start(bf16[256,256]{1,0:T(8,128)(2,1)S(1)} %get-tuple-element.154), channel_id=1, source_target_pairs={{0,2},{1,3},{2,0},{3,1},{4,6},{5,7},{6,4},{7,5},{8,10},{9,11},{10,... | collective-permute-start | bytes 393224 | tf_op jit(solution)/shard_map/ppermute | solution.py:647
